TPU v7x, 128 devices: a whole 4x4x4 slice. The times are simulated.
128 devices in a mesh: rep: 1, dp: 128 (over z, y, x, core).
Axes of the slice: x: 4, y: 4, z: 4, core: 2. Of those that a mesh axis runs over, the one named last changes fastest.
Arguments:
- hidden: bfloat16 [256, 2048], P(('rep', 'dp'))
- lengths: int32 [256], P(('rep', 'dp'))
- kv_cache: bfloat16 [2, 256, 512, 576], P(None, ('rep', 'dp'))
- norm_attn: float32 [2, 2048], replicated
- w_q: bfloat16 [2, 2048, 11520], replicated
- w_o: bfloat16 [2, 10240, 2048], replicated
- norm_ffn: float32 [2, 2048], replicated
- w_gate: bfloat16 [2, 2048, 10240], P(None, None, 'dp')
- w_up: bfloat16 [2, 2048, 10240], P(None, None, 'dp')
- w_down: bfloat16 [2, 10240, 2048], P(None, 'dp')
- norm_final: float32 [2048], replicated
- w_head: bfloat16 [2048, 154880], P(None, 'dp')
Outputs:
- output: float32 [256, 154880], P('rep', 'dp')
All inputs are finite; a program needn't handle non-finite values.
Results may differ from a plain program's by a relative error of at most 0.02.
Values are sent between devices in bfloat16 or wider.
A program may use at most 1 GiB of HBM per device.

v0:
```python
import jax
import jax.numpy as jnp
from jax import lax
from jax.sharding import PartitionSpec as P

LATENT_DIM = 512
QK_SCALE = 192 ** -0.5
NORM_EPS = 1e-6


def rms_norm(x_rows, gain_vec):
    x_float = x_rows.astype(jnp.float32)
    inv_rms = lax.rsqrt(jnp.mean(x_float * x_float, axis=-1, keepdims=True) + NORM_EPS)
    return (x_float * inv_rms * gain_vec).astype(jnp.bfloat16)


def mla_attention(normed, w_q, kv_cache, lengths):
    num_rows, seq_len, kv_width = kv_cache.shape
    q_heads = jnp.dot(normed, w_q, preferred_element_type=jnp.float32).astype(jnp.bfloat16)
    q_heads = q_heads.reshape(num_rows, -1, kv_width)
    scores = jnp.einsum('bhc,btc->bht', q_heads, kv_cache, preferred_element_type=jnp.float32) * QK_SCALE
    key_pos = lax.broadcasted_iota(jnp.int32, (1, 1, seq_len), 2)
    scores = jnp.where(key_pos < lengths[:, None, None], scores, -1e30)
    attn_probs = jax.nn.softmax(scores, axis=-1).astype(jnp.bfloat16)
    context = jnp.einsum('bht,btc->bhc', attn_probs, kv_cache[:, :, :LATENT_DIM], preferred_element_type=jnp.float32)
    return context.astype(jnp.bfloat16).reshape(num_rows, -1)


def ffn_block(normed, w_gate, w_up, w_down):
    gate_proj = jnp.dot(normed, w_gate, preferred_element_type=jnp.float32)
    up_proj = jnp.dot(normed, w_up, preferred_element_type=jnp.float32)
    act_rows = (jax.nn.silu(gate_proj) * up_proj).astype(jnp.bfloat16)
    return jnp.dot(act_rows, w_down, preferred_element_type=jnp.float32)


def add_residual(x_rows, delta):
    return (x_rows.astype(jnp.float32) + delta).astype(jnp.bfloat16)


def solution(mesh):
    row_axes = ('rep', 'dp')
    specs_in = (P(row_axes, None), P(row_axes), P(None, row_axes, None, None), P(), P(), P(), P(),
                P(None, None, 'dp'), P(None, None, 'dp'), P(None, 'dp', None), P(), P(None, 'dp'))

    def device_step(hidden, lengths, kv_cache, norm_attn, w_q, w_o, norm_ffn, w_gate, w_up, w_down, norm_final, w_head):
        x_rows = hidden
        for layer_idx in range(kv_cache.shape[0]):
            normed = rms_norm(x_rows, norm_attn[layer_idx])
            context = mla_attention(normed, w_q[layer_idx], kv_cache[layer_idx], lengths)
            x_rows = add_residual(x_rows, jnp.dot(context, w_o[layer_idx], preferred_element_type=jnp.float32))
            normed = rms_norm(x_rows, norm_ffn[layer_idx])
            gathered = lax.all_gather(normed, 'dp', axis=0, tiled=True)
            part_sum = ffn_block(gathered, w_gate[layer_idx], w_up[layer_idx], w_down[layer_idx])
            ffn_out = lax.psum_scatter(part_sum, 'dp', scatter_dimension=0, tiled=True)
            x_rows = add_residual(x_rows, ffn_out)
        normed = rms_norm(x_rows, norm_final)
        gathered = lax.all_gather(normed, 'dp', axis=0, tiled=True)
        return jnp.dot(gathered, w_head, preferred_element_type=jnp.float32)

    return jax.shard_map(device_step, mesh=mesh, in_specs=specs_in, out_specs=P('rep', 'dp'), check_vma=False)
```

profile of v0, /device:TPU:1, one launch (start us, length us, event | category | flops | bytes accessed | tf_op | source)
XLA Modules:
  0.0 608.2 jit_solution(4947163921665170593)
XLA Ops:
  6.5 2.9 slice_bitcast_fusion.1
  9.6 17.1 %fusion.14 = bf16[2,11520]{1,0:T(2,128)(2,1)} fusion(bf16[2,2048,11520]{2,1,0:T(8,128)(2,1)} %param.16, bf16[2,2048]{1,0:T(2,128)(2,1)S(1)} %copy-done.7, f32[2]{0:T(128)S(1)} %add_rsqrt_fusion.4, f32[2048]{0:T(1024)S(1)} %bitcast.91), kind=kOutput, calls=%fused_computation.14 | convolution fusion | flops 94411264 | bytes 47248392 | tf_op jit(solution)/shard_map/dot_general | solution.py:19
  26.7 1.5 reshape.78
  28.3 0.7 iota_compare_fusion
  29.0 1.1 fusion.43
  30.7 0.8 fusion.108
  31.5 2.0 fusion.46
  33.5 0.8 copy.21
  34.3 1.4 fusion.106
  35.7 15.3 %multiply_reduce_fusion.1 = (f32[2]{0:T(128)S(1)}, f32[2,2048]{1,0:T(2,128)S(1)}) fusion(bf16[2,10240]{1,0:T(2,128)(2,1)S(1)} %bitcast.88, bf16[2,10240,2048]{2,1,0:T(8,128)(2,1)} %param.17, bf16[2,2048]{1,0:T(2,128)(2,1)S(1)} %copy-done.7), kind=kOutput, calls=%fused_computation.96 | convolution fusion | flops 83910656 | bytes 42008584 | tf_op jit(solution)/shard_map/dot_general | solution.py:50
  51.0 0.7 fusion.100
  51.8 67.3 %all-gather.7.cloned.1.call-done = bf16[128,2,2048]{2,1,0:T(2,128)(2,1)} async-done(((bf16[1,2,2048]{2,1,0:T(2,128)(2,1)}), bf16[128,2,2048]{2,1,0:T(2,128)(2,1)}) %all-gather.7.cloned.1.call-update) | async-done | bytes 1048592 | tf_op jit(solution)/shard_map/all_gather | solution.py:52
  119.1 1.5 reshape.83
  120.5 1.4 fusion.60
  122.0 3.8 fusion.49
  125.8 149.2 %all-reduce.5.cloned.1.call-done = f32[256,2048]{1,0:T(8,128)} async-done(((f32[256,2048]{1,0:T(8,128)}), f32[256,2048]{1,0:T(8,128)}) %all-reduce.5.cloned.1.call-update) | async-done | bytes 2097168
  275.0 1.0 fusion.90
  276.0 17.1 %fusion.17 = bf16[2,11520]{1,0:T(2,128)(2,1)} fusion(bf16[2,2048,11520]{2,1,0:T(8,128)(2,1)} %param.16, bf16[2,2048]{1,0:T(2,128)(2,1)S(1)} %get-tuple-element.8, f32[2]{0:T(128)S(1)} %add_rsqrt_fusion.2, f32[2048]{0:T(1024)S(1)} %bitcast.90), kind=kOutput, calls=%fused_computation.15 | convolution fusion | flops 94411264 | bytes 47248392 | tf_op jit(solution)/shard_map/dot_general | solution.py:19
  293.1 1.5 reshape.80
  294.6 1.1 fusion.42
  296.5 1.4 fusion.47
  298.0 15.3 %multiply_reduce_fusion = (f32[2]{0:T(128)S(1)}, f32[2,2048]{1,0:T(2,128)S(1)}) fusion(bf16[2,10240]{1,0:T(2,128)(2,1)S(1)} %bitcast.89, bf16[2,10240,2048]{2,1,0:T(8,128)(2,1)} %param.17, bf16[2,2048]{1,0:T(2,128)(2,1)S(1)} %get-tuple-element.8), kind=kOutput, calls=%fused_computation.94 | convolution fusion | flops 83910656 | bytes 42008584 | tf_op jit(solution)/shard_map/dot_general | solution.py:50
  313.3 0.7 fusion.101
  314.1 62.4 %all-gather.9.cloned.1.call-done = bf16[128,2,2048]{2,1,0:T(2,128)(2,1)} async-done(((bf16[1,2,2048]{2,1,0:T(2,128)(2,1)}), bf16[128,2,2048]{2,1,0:T(2,128)(2,1)}) %all-gather.9.cloned.1.call-update) | async-done | bytes 1048592 | tf_op jit(solution)/shard_map/all_gather | solution.py:52
  376.4 1.5 reshape.85
  378.4 2.7 fusion.48
  381.2 149.2 %all-reduce.7.cloned.1.call-done = f32[256,2048]{1,0:T(8,128)} async-done(((f32[256,2048]{1,0:T(8,128)}), f32[256,2048]{1,0:T(8,128)}) %all-reduce.7.cloned.1.call-update) | async-done | bytes 2097168
  530.3 1.0 fusion.84
  531.3 0.7 fusion.99
  532.0 63.2 %all-gather.11.cloned.1.call-done = bf16[128,2,2048]{2,1,0:T(2,128)(2,1)} async-done(((bf16[1,2,2048]{2,1,0:T(2,128)(2,1)}), bf16[128,2,2048]{2,1,0:T(2,128)(2,1)}) %all-gather.11.cloned.1.call-update) | async-done | bytes 1048592 | tf_op jit(solution)/shard_map/all_gather | solution.py:57
  595.3 1.5 reshape.87
  596.7 4.9 fusion.110
  (44 shorter events, 2.4 us)
Async XLA Ops:
  6.5 2.9 copy-start.7
  6.5 3.0 copy-start.10
  6.5 112.5 %all-gather.7.cloned.1.call-start = ((), (), s32[]{:S(2)}) async-start(), calls=%async_computation | async-start | bytes 1056768 | tf_op jit(solution)/shard_map/all_gather | solution.py:52
  9.6 19.4 %copy-start = (bf16[2,2,512,576]{2,3,1,0:T(8,128)(2,1)S(1)}, bf16[2,2,512,576]{2,3,1,0:T(8,128)(2,1)}, u32[]{:S(2)}) copy-start(bf16[2,2,512,576]{2,3,1,0:T(8,128)(2,1)} %param.14) | copy-start | bytes 7077892
  29.0 2.5 copy-start.9
  30.1 0.6 copy-start.6
  51.7 223.3 %all-reduce.5.cloned.1.call-start = ((), (), s32[]{:S(2)}) async-start(), calls=%async_computation.3 | async-start | bytes 4194304
  125.7 250.7 %all-gather.9.cloned.1.call-start = ((), (), s32[]{:S(2)}) async-start(), calls=%async_computation.1 | async-start | bytes 1056768 | tf_op jit(solution)/shard_map/all_gather | solution.py:52
  276.0 20.5 %copy-start.1 = (bf16[2,512,576]{1,2,0:T(8,128)(2,1)S(1)}, bf16[2,512,576]{1,2,0:T(8,128)(2,1)}, u32[]{:S(2)}) copy-start(bf16[2,512,576]{1,2,0:T(8,128)(2,1)} %get-tuple-element.10) | copy-start | bytes 3538948
  295.7 0.6 copy-start.5
  297.9 15.4 %copy-start.8 = (f32[1,2048]{1,0:T(1,128)S(1)}, f32[1,2048]{1,0:T(1,128)}, u32[]{:S(2)}) copy-start(f32[1,2048]{1,0:T(1,128)} %get-tuple-element.11) | copy-start | bytes 24580
  297.9 80.0 %copy-start.2 = (bf16[2,2048,80]{1,2,0:T(8,128)(2,1)S(1)}, bf16[2,2048,80]{1,2,0:T(8,128)(2,1)}, u32[]{:S(2)}) copy-start(bf16[2,2048,80]{1,2,0:T(8,128)(2,1)} %param.19) | copy-start | bytes 1966084
  313.3 65.1 %copy-start.3 = (bf16[2,80,2048]{2,1,0:T(8,128)(2,1)S(1)}, bf16[2,80,2048]{2,1,0:T(8,128)(2,1)}, u32[]{:S(2)}) copy-start(bf16[2,80,2048]{2,1,0:T(8,128)(2,1)} %param.21) | copy-start | bytes 1966084
  313.3 65.1 %copy-start.4 = (bf16[2,2048,80]{1,2,0:T(8,128)(2,1)S(1)}, bf16[2,2048,80]{1,2,0:T(8,128)(2,1)}, u32[]{:S(2)}) copy-start(bf16[2,2048,80]{1,2,0:T(8,128)(2,1)} %param.20) | copy-start | bytes 1966084
  314.0 216.3 %all-reduce.7.cloned.1.call-start = ((), (), s32[]{:S(2)}) async-start(), calls=%async_computation.4 | async-start | bytes 4194304
  378.4 152.9 %copy-start.11 = (f32[2048]{0:T(1024)S(1)}, f32[2048]{0:T(1024)}, u32[]{:S(2)}) copy-start(f32[2048]{0:T(1024)} %param.22) | copy-start | bytes 24580
  381.1 214.1 %all-gather.11.cloned.1.call-start = ((), (), s32[]{:S(2)}) async-start(), calls=%async_computation.2 | async-start | bytes 1056768 | tf_op jit(solution)/shard_map/all_gather | solution.py:57
Sparse Core Ops, SparseCore 0:
  51.8 67.1 all-gather.6
  125.9 149.0 all-reduce.4
  314.2 62.2 all-gather.8
  381.2 149.0 all-reduce.6
  533.0 62.2 all-gather.10
where the time goes:
time: 609 us; the launch traced here: 608 us
  waiting for transfers between devices  491 us (81%)
  matrix products  83.6 us (14%)
  local copies, waits for them, and re-layouts  13.9 us (2%)
  between operations  13.3 us (2%)
    unnamed x7, waiting for transfers between devices  298 us
    all_gather x3, waiting for transfers between devices, device_step(): gathered = lax.all_gather(normed, 'dp', axis=0, tiled=True)  193 us
    dot_general x2, matrix products, mla_attention(): jnp.dot(normed, w_q, preferred_element_type=jnp.float32)  34.2 us
    dot_general x2, matrix products, device_step(): jnp.dot(context, w_o[layer_idx], preferred_element_type=jnp.float32)  30.6 us
  transfers between devices with their start and end apart: 5, of which 5 were waited for; matrix products, arithmetic and copies ran while one was open for 0% of the time, Pallas kernels for 0%

commit v1 on v0

--- a/solution.py
+++ b/solution.py
@@ -1,11 +1,17 @@
+import functools
+
 import jax
 import jax.numpy as jnp
 from jax import lax
+from jax.experimental import pallas as pl
+from jax.experimental.pallas import tpu as pltpu
 from jax.sharding import PartitionSpec as P
 
 LATENT_DIM = 512
 QK_SCALE = 192 ** -0.5
 NORM_EPS = 1e-6
+MESH = pl.DeviceIdType.MESH
+VMEM_LIMIT = 60 * 1024 * 1024
 
 
 def rms_norm(x_rows, gain_vec):
@@ -37,8 +43,87 @@
     return (x_rows.astype(jnp.float32) + delta).astype(jnp.bfloat16)
 
 
+def all_barrier(me, n):
+    barrier = pltpu.get_barrier_semaphore()
+
+    def signal(i, carry):
+        pl.semaphore_signal(barrier, inc=1, device_id={'dp': lax.rem(me + i, n)}, device_id_type=MESH)
+        return carry
+
+    lax.fori_loop(1, n, signal, 0)
+    pl.semaphore_wait(barrier, n - 1)
+
+
+def gather_kernel(n, block_ref, out_ref, send_sem, recv_sem):
+    me = lax.axis_index('dp')
+    all_barrier(me, n)
+
+    def send(i, carry):
+        peer = lax.rem(me + i, n)
+        pltpu.make_async_remote_copy(block_ref, out_ref.at[me], send_sem, recv_sem,
+                                     device_id={'dp': peer}, device_id_type=MESH).start()
+        return carry
+
+    lax.fori_loop(1, n, send, 0)
+    out_ref[me] = block_ref[...]
+    others = out_ref.at[pl.ds(0, n - 1)]
+    pltpu.make_async_copy(others, others, recv_sem).wait()
+    pltpu.make_async_copy(others, others, send_sem).wait()
+
+
+def scatter_kernel(n, part_ref, out_ref, land, send_sem, recv_sem):
+    me = lax.axis_index('dp')
+    all_barrier(me, n)
+
+    def send(i, carry):
+        peer = lax.rem(me + i, n)
+        pltpu.make_async_remote_copy(part_ref.at[peer], land.at[me], send_sem, recv_sem,
+                                     device_id={'dp': peer}, device_id_type=MESH).start()
+        return carry
+
+    lax.fori_loop(1, n, send, 0)
+    land[me] = part_ref[me]
+    others = land.at[pl.ds(0, n - 1)]
+    pltpu.make_async_copy(others, others, recv_sem).wait()
+
+    def add(i, total):
+        return total + land[i]
+
+    out_ref[...] = lax.fori_loop(1, n, add, land[0])
+    pltpu.make_async_copy(others, others, send_sem).wait()
+
+
+def comm_params(collective_id):
+    return pltpu.CompilerParams(collective_id=collective_id, has_side_effects=True, vmem_limit_bytes=VMEM_LIMIT)
+
+
+def gather_rows(block, n):
+    rows, cols = block.shape
+    return pl.pallas_call(
+        functools.partial(gather_kernel, n),
+        out_shape=jax.ShapeDtypeStruct((n, rows, cols), block.dtype),
+        in_specs=[pl.BlockSpec(memory_space=pltpu.VMEM)],
+        out_specs=pl.BlockSpec(memory_space=pltpu.VMEM),
+        scratch_shapes=[pltpu.SemaphoreType.DMA, pltpu.SemaphoreType.DMA],
+        compiler_params=comm_params(0),
+    )(block).reshape(n * rows, cols)
+
+
+def scatter_rows(part, n):
+    rows, cols = part.shape[0] // n, part.shape[1]
+    return pl.pallas_call(
+        functools.partial(scatter_kernel, n),
+        out_shape=jax.ShapeDtypeStruct((rows, cols), part.dtype),
+        in_specs=[pl.BlockSpec(memory_space=pltpu.VMEM)],
+        out_specs=pl.BlockSpec(memory_space=pltpu.VMEM),
+        scratch_shapes=[pltpu.VMEM((n, rows, cols), part.dtype), pltpu.SemaphoreType.DMA, pltpu.SemaphoreType.DMA],
+        compiler_params=comm_params(1),
+    )(part.reshape(n, rows, cols))
+
+
 def solution(mesh):
     row_axes = ('rep', 'dp')
+    n = mesh.shape['dp']
     specs_in = (P(row_axes, None), P(row_axes), P(None, row_axes, None, None), P(), P(), P(), P(),
                 P(None, None, 'dp'), P(None, None, 'dp'), P(None, 'dp', None), P(), P(None, 'dp'))
 
@@ -49,12 +134,11 @@
             context = mla_attention(normed, w_q[layer_idx], kv_cache[layer_idx], lengths)
             x_rows = add_residual(x_rows, jnp.dot(context, w_o[layer_idx], preferred_element_type=jnp.float32))
             normed = rms_norm(x_rows, norm_ffn[layer_idx])
-            gathered = lax.all_gather(normed, 'dp', axis=0, tiled=True)
+            gathered = gather_rows(normed, n)
             part_sum = ffn_block(gathered, w_gate[layer_idx], w_up[layer_idx], w_down[layer_idx])
-            ffn_out = lax.psum_scatter(part_sum, 'dp', scatter_dimension=0, tiled=True)
-            x_rows = add_residual(x_rows, ffn_out)
+            x_rows = add_residual(x_rows, scatter_rows(part_sum, n))
         normed = rms_norm(x_rows, norm_final)
-        gathered = lax.all_gather(normed, 'dp', axis=0, tiled=True)
+        gathered = gather_rows(normed, n)
         return jnp.dot(gathered, w_head, preferred_element_type=jnp.float32)
 
     return jax.shard_map(device_step, mesh=mesh, in_specs=specs_in, out_specs=P('rep', 'dp'), check_vma=False)

time: 609 us -> 265 us (0.44)
  waiting for transfers between devices: 491 us -> 0 us
  Pallas kernels: 0 us -> 158 us
  between operations: 13.3 us -> 0.26 us
    unnamed x7 -> x0, waiting for transfers between devices: 298 us -> none
    all_gather x3 -> x0, waiting for transfers between devices: 193 us -> none  [device_step(): gathered = lax.all_gather(normed, 'dp', axis=0, tiled=True)]
    pallas_call x0 -> x5, Pallas kernels: none -> 158 us  [the longest x2 81.7 us: scatter_rows(): pl.pallas_call(functools.partial(scatter_kernel, n), out_shape=jax.ShapeD...]
  transfers between devices with their start and end apart: 5 -> 0, of which waited for: 5 -> 0; matrix products, arithmetic and copies ran while one was open for 0% -> 0% of each run, Pallas kernels for 0% -> 0%
where the time goes in v1:
time: 265 us; the launch traced here: 264 us
  Pallas kernels  158 us (60%)
  matrix products  80.5 us (30%)
  local copies, waits for them, and re-layouts  18.8 us (7%)
  other arithmetic  6.25 us (2%)
    pallas_call x2, Pallas kernels, scatter_rows(): pl.pallas_call(functools.partial(scatter_kernel, n), out_shape=jax.ShapeD...  81.7 us
    pallas_call x3, Pallas kernels, gather_rows(): pl.pallas_call(functools.partial(gather_kernel, n), out_shape=jax.ShapeDt...  76.1 us
    dot_general x2, matrix products, mla_attention(): jnp.dot(normed, w_q, preferred_element_type=jnp.float32)  34.1 us
    dot_general x2, matrix products, device_step(): jnp.dot(context, w_o[layer_idx], preferred_element_type=jnp.float32)  30.5 us
    dot_general x2, local copies, waits for them, and re-layouts, ffn_block(): return jnp.dot(act_rows, w_down, preferred_element_type=jnp.float32)  5.94 us

profile of v1, /device:TPU:1, one launch (start us, length us, event | category | flops | bytes accessed | tf_op | source)
XLA Modules:
  0.0 263.6 jit_solution(4505882451692755505)
XLA Ops:
  0.0 0.8 fusion.73
  0.8 0.7 iota_compare_fusion
  1.6 0.8 fusion.84
  2.4 1.4 fusion.83
  3.8 17.0 %fusion.14 = bf16[2,11520]{1,0:T(2,128)(2,1)S(1)} fusion(bf16[2,2048,11520]{2,1,0:T(8,128)(2,1)} %param.16, bf16[2,2048]{1,0:T(2,128)(2,1)} %param.12, f32[2]{0:T(128)S(1)} %add_rsqrt_fusion.4, f32[2048]{0:T(1024)S(1)} %bitcast.89), kind=kOutput, calls=%fused_computation.14 | convolution fusion | flops 94411264 | bytes 47248392 | tf_op jit(solution)/shard_map/dot_general | solution.py:25
  21.9 0.7 fusion.85
  22.6 1.2 slice_bitcast_fusion.1
  23.8 2.0 fusion.46
  25.8 0.8 copy.29
  26.7 15.3 %multiply_reduce_fusion.1 = (f32[2]{0:T(128)S(1)}, f32[2,2048]{1,0:T(2,128)S(1)}) fusion(bf16[2,10240]{1,0:T(2,128)(2,1)S(1)} %bitcast.87, bf16[2,10240,2048]{2,1,0:T(8,128)(2,1)} %param.17, bf16[2,2048]{1,0:T(2,128)(2,1)S(1)} %copy-done.6), kind=kOutput, calls=%fused_computation.84 | convolution fusion | flops 83910656 | bytes 42008584 | tf_op jit(solution)/shard_map/dot_general | solution.py:135
  42.6 27.3 %shard_map.118 = bf16[128,2,2048]{2,1,0:T(2,128)(2,1)} custom-call(bf16[2,2048]{1,0:T(2,128)(2,1)} %multiply_convert_fusion.1.block_ref), custom_call_target="tpu_custom_call" | custom-call | tf_op jit(solution)/shard_map/pallas_call | solution.py:102
  69.9 1.5 reshape.93
  71.4 1.4 fusion.58
  72.8 2.0 fusion.44
  74.9 0.9 copy.20
  75.7 1.4 fusion.55
  77.1 3.0 %copy.22.part_ref = f32[128,2,2048]{2,1,0:T(2,128)} copy(f32[128,2,2048]{2,0,1:T(8,128)S(1)} %fusion.55) | data formatting | bytes 4194304 | tf_op jit(solution)/shard_map/dot_general | solution.py:39
  80.1 39.3 %shard_map.119 = f32[2,2048]{1,0:T(2,128)} custom-call(f32[128,2,2048]{2,1,0:T(2,128)} %copy.22.part_ref), custom_call_target="tpu_custom_call" | custom-call | tf_op jit(solution)/shard_map/pallas_call | solution.py:114
  119.4 0.8 fusion.76
  120.3 17.1 %fusion.17 = bf16[2,11520]{1,0:T(2,128)(2,1)} fusion(bf16[2,2048,11520]{2,1,0:T(8,128)(2,1)} %param.16, bf16[2,2048]{1,0:T(2,128)(2,1)S(1)} %get-tuple-element.8, f32[2]{0:T(128)S(1)} %add_rsqrt_fusion.2, f32[2048]{0:T(1024)S(1)} %bitcast.88), kind=kOutput, calls=%fused_computation.15 | convolution fusion | flops 94411264 | bytes 47248392 | tf_op jit(solution)/shard_map/dot_general | solution.py:25
  137.4 1.5 reshape.94
  138.9 1.1 fusion.42
  140.8 1.4 fusion.47
  142.3 15.3 %multiply_reduce_fusion = (f32[2]{0:T(128)S(1)}, f32[2,2048]{1,0:T(2,128)S(1)}) fusion(bf16[2,10240]{1,0:T(2,128)(2,1)S(1)} %bitcast.86, bf16[2,10240,2048]{2,1,0:T(8,128)(2,1)} %param.17, bf16[2,2048]{1,0:T(2,128)(2,1)S(1)} %get-tuple-element.8), kind=kOutput, calls=%fused_computation.81 | convolution fusion | flops 83910656 | bytes 42008584 | tf_op jit(solution)/shard_map/dot_general | solution.py:135
  158.2 25.5 %shard_map.120 = bf16[128,2,2048]{2,1,0:T(2,128)(2,1)} custom-call(bf16[2,2048]{1,0:T(2,128)(2,1)} %multiply_convert_fusion.block_ref), custom_call_target="tpu_custom_call" | custom-call | tf_op jit(solution)/shard_map/pallas_call | solution.py:102
  183.7 1.7 reshape.96
  186.9 3.0 %copy.26.part_ref = f32[128,2,2048]{2,1,0:T(2,128)} copy(f32[128,2,2048]{2,0,1:T(8,128)S(1)} %fusion.50) | data formatting | bytes 4194304 | tf_op jit(solution)/shard_map/dot_general | solution.py:39
  189.9 42.4 %shard_map.121 = f32[2,2048]{1,0:T(2,128)} custom-call(f32[128,2,2048]{2,1,0:T(2,128)} %copy.26.part_ref), custom_call_target="tpu_custom_call" | custom-call | tf_op jit(solution)/shard_map/pallas_call | solution.py:114
  232.2 0.8 fusion.70
  233.8 23.4 %shard_map.122 = bf16[128,2,2048]{2,1,0:T(2,128)(2,1)} custom-call(bf16[2,2048]{1,0:T(2,128)(2,1)} %fusion.72.block_ref), custom_call_target="tpu_custom_call" | custom-call | tf_op jit(solution)/shard_map/pallas_call | solution.py:102
  257.2 1.5 reshape.97
  258.7 4.9 %fusion.87 = f32[256,1210]{0,1:T(8,128)} fusion(bf16[256,2048]{1,0:T(8,128)(2,1)S(1)} %reshape.97, bf16[2048,1210]{0,1:T(8,128)(2,1)} %param.23), kind=kOutput, calls=%fused_computation.97 | convolution fusion | flops 1268776960 | bytes 7243776 | tf_op jit(solution)/shard_map/dot_general | solution.py:142
  (40 shorter events, 5.4 us)
Async XLA Ops:
  1.6 19.4 %copy-start.9 = (pred[2,512]{1,0:T(4,128)(4,1)}, pred[2,512]{1,0:T(4,128)(4,1)S(1)}, u32[]{:S(2)}) copy-start(pred[2,512]{1,0:T(4,128)(4,1)S(1)} %iota_compare_fusion) | copy-start | bytes 3076
  3.8 17.2 %copy-start = (bf16[2,2,512,576]{2,3,1,0:T(8,128)(2,1)S(1)}, bf16[2,2,512,576]{2,3,1,0:T(8,128)(2,1)}, u32[]{:S(2)}) copy-start(bf16[2,2,512,576]{2,3,1,0:T(8,128)(2,1)} %param.14) | copy-start | bytes 7077892
  21.2 0.6 copy-start.4
  22.6 4.1 %copy-start.6 = (bf16[2,2048]{1,0:T(2,128)(2,1)S(1)}, bf16[2,2048]{1,0:T(2,128)(2,1)}, u32[]{:S(2)}) copy-start(bf16[2,2048]{1,0:T(2,128)(2,1)} %param.12) | copy-start | bytes 24580
  26.7 15.3 %copy-start.8 = (f32[1,2048]{1,0:T(1,128)S(1)}, f32[1,2048]{1,0:T(1,128)}, u32[]{:S(2)}) copy-start(f32[1,2048]{1,0:T(1,128)} %get-tuple-element.12) | copy-start | bytes 24580
  120.3 20.5 %copy-start.1 = (bf16[2,512,576]{1,2,0:T(8,128)(2,1)S(1)}, bf16[2,512,576]{1,2,0:T(8,128)(2,1)}, u32[]{:S(2)}) copy-start(bf16[2,512,576]{1,2,0:T(8,128)(2,1)} %get-tuple-element.10) | copy-start | bytes 3538948
  140.0 0.6 copy-start.5
  142.3 15.3 %copy-start.7 = (f32[1,2048]{1,0:T(1,128)S(1)}, f32[1,2048]{1,0:T(1,128)}, u32[]{:S(2)}) copy-start(f32[1,2048]{1,0:T(1,128)} %get-tuple-element.11) | copy-start | bytes 24580
  157.5 27.9 %copy-start.3 = (bf16[2,2048,80]{1,2,0:T(8,128)(2,1)S(1)}, bf16[2,2048,80]{1,2,0:T(8,128)(2,1)}, u32[]{:S(2)}) copy-start(bf16[2,2048,80]{1,2,0:T(8,128)(2,1)} %param.19) | copy-start | bytes 1966084
  157.5 28.3 %copy-start.11 = (bf16[2,2048,80]{1,2,0:T(8,128)(2,1)S(1)}, bf16[2,2048,80]{1,2,0:T(8,128)(2,1)}, u32[]{:S(2)}) copy-start(bf16[2,2048,80]{1,2,0:T(8,128)(2,1)} %param.20) | copy-start | bytes 1966084
  183.7 2.7 %copy-start.2 = (bf16[2,80,2048]{2,1,0:T(8,128)(2,1)S(1)}, bf16[2,80,2048]{2,1,0:T(8,128)(2,1)}, u32[]{:S(2)}) copy-start(bf16[2,80,2048]{2,1,0:T(8,128)(2,1)} %param.21) | copy-start | bytes 1966084
  186.9 46.2 %copy-start.10 = (f32[2048]{0:T(1024)S(1)}, f32[2048]{0:T(1024)}, u32[]{:S(2)}) copy-start(f32[2048]{0:T(1024)} %param.22) | copy-start | bytes 24580

commit v2 on v0

v2 whole, which is shorter than its diff:
```python
import jax
import jax.numpy as jnp
from jax import lax
from jax.experimental import pallas as pl
from jax.experimental.pallas import tpu as pltpu
from jax.sharding import PartitionSpec as P

MESH = pl.DeviceIdType.MESH
QK_SCALE = 192 ** -0.5
NORM_EPS = 1e-6

LAYERS = 2
ROWS = 2
TEAM = 8
TEAMS = 16
TEAM_ROWS = ROWS * TEAM
ALL_ROWS = TEAM_ROWS * TEAMS
D = 2048
D_OWN = D // TEAM
HEADS = 20
LATENT = 512
KV = 576
SEQ = 512
Q_COLS = HEADS * KV
Q_OWN = 1536
Q_LAST = Q_COLS - Q_OWN
PAIR = 2 * KV
PAIRS = HEADS // 2
SHIFT = 64
WIDE = KV + SHIFT
O_ROWS = 48
F_OWN = 80
F_TEAM = F_OWN * TEAM
F32 = jnp.float32
BF16 = jnp.bfloat16


def norm_rows(x, gain):
    inv_rms = lax.rsqrt(jnp.mean(x * x, axis=-1, keepdims=True) + NORM_EPS)
    return (x * inv_rms * gain).astype(BF16)


def dot_f32(a, b, contract=((1,), (0,))):
    return lax.dot_general(a, b, (contract, ((), ())), preferred_element_type=F32)


def wait_bytes(ref, sem):
    pltpu.make_async_copy(ref, ref, sem).wait()


def q_segments():
    pieces = []
    for pair in range(PAIRS):
        at, end = pair * PAIR, (pair + 1) * PAIR
        while at < end:
            sender = at // Q_OWN
            first = min(sender * Q_OWN, Q_LAST)
            stop = min(end, (sender + 1) * Q_OWN, Q_COLS)
            pieces.append((pair, at - pair * PAIR, sender, at - first, stop - at))
            at = stop
    return pieces


def decode_kernel(hidden, lengths, kv_cache, norm_attn, w_q, w_o, norm_ffn, w_gate, w_up, w_down, norm_final,
                  out, pack, spread, hid_send, hid_land, x_team, xb_team, wq_buf, kv_buf, wo_buf, wgu_buf, wd_buf,
                  q_send, q_land, q_pairs, o_send, o_land, o_heads, x_all, g_buf, a_all, part, land,
                  load_sem, entry_sem, send_sem, recv_sem, plane_sem, down_send, down_recv):
    me = lax.axis_index('dp')
    team, slot = me // TEAM, lax.rem(me, TEAM)
    plane, core = team // 4, lax.rem(me, 2)
    sibling = me + 1 - 2 * core
    own_cols = pl.ds(pl.multiple_of(slot * D_OWN, D_OWN), D_OWN)
    q_start = pl.multiple_of(jnp.minimum(slot * Q_OWN, Q_LAST), 128)

    def mate(i):
        return team * TEAM + lax.rem(slot + i, TEAM)

    def remote(src, dst, ssem, rsem, device):
        return pltpu.make_async_remote_copy(src, dst, ssem, rsem, device_id={'dp': device}, device_id_type=MESH)

    barrier = pltpu.get_barrier_semaphore()
    for i in range(1, TEAM):
        pl.semaphore_signal(barrier, inc=1, device_id={'dp': mate(i)}, device_id_type=MESH)

    def greet(i, carry):
        pl.semaphore_signal(barrier, inc=1, device_id={'dp': lax.rem(me + i * TEAM, TEAM * TEAMS)}, device_id_type=MESH)
        return carry

    lax.fori_loop(1, TEAMS, greet, 0)

    loads = []
    for layer in range(LAYERS):
        batch = [
            (w_q.at[layer, :, pl.ds(q_start, Q_OWN)], wq_buf.at[layer]),
            (kv_cache.at[layer], kv_buf.at[layer, :, pl.ds(SHIFT, KV)]),
            (w_o.at[layer, :, own_cols], wo_buf.at[layer]),
            (w_gate.at[layer], wgu_buf.at[layer, pl.ds(0, F_OWN)]),
            (w_up.at[layer], wgu_buf.at[layer, pl.ds(F_OWN, F_OWN)]),
            (w_down.at[layer, :, own_cols], wd_buf.at[layer, pl.ds(pl.multiple_of(slot * F_OWN, 16), F_OWN)]),
        ]
        loads.append([pltpu.make_async_copy(src, dst, load_sem.at[layer, i]) for i, (src, dst) in enumerate(batch)])
    for batch in loads:
        for copy in batch:
            copy.start()

    for layer in range(LAYERS):
        for r in range(ROWS):
            kv_buf[layer, r, 0:SHIFT, :] = jnp.zeros((SHIFT, SEQ), BF16)
            kv_buf[layer, r, SHIFT + KV:, :] = jnp.zeros((SHIFT, SEQ), BF16)
    q_pairs[...] = jnp.zeros_like(q_pairs)
    make_selectors(pack, spread)
    hid_send[...] = hidden[...].astype(F32)
    hid_land[slot] = hid_send[...]

    pl.semaphore_wait(barrier, TEAM - 1 + TEAMS - 1)
    for i in range(1, TEAM):
        pl.semaphore_signal(entry_sem, inc=1, device_id={'dp': mate(i)}, device_id_type=MESH)

    def gather_team(src, dst, sem):
        for i in range(1, TEAM):
            remote(src, dst, send_sem.at[sem], recv_sem.at[sem], mate(i)).start()

    def gather_all(block, step):
        dst = x_all.at[step]
        mine = dst.at[team, :, own_cols]
        mine[...] = block
        sem = 16 + 2 * step
        for dz in range(4):
            to_plane = lax.rem(plane + dz, 4)

            def send(i, carry):
                spot = lax.rem(lax.rem(me, 32) // 2 + i, 16)
                remote(mine, mine, send_sem.at[sem], plane_sem.at[step, (4 - dz) % 4],
                       to_plane * 32 + spot * 2 + core).start()
                return carry

            lax.fori_loop(1 if dz == 0 else 0, 16, send, 0)
        for dz in range(4):
            from_plane = lax.rem(plane + dz, 4)
            if dz == 0:
                wait_bytes(dst.at[0:3, :, 0:5 * D_OWN], plane_sem.at[step, dz])
            else:
                wait_bytes(dst.at[0:4, :, 0:4 * D_OWN], plane_sem.at[step, dz])
            for x in range(4):
                cols = pl.ds(pl.multiple_of((2 * x + core) * D_OWN, D_OWN), D_OWN)
                piece = dst.at[pl.ds(from_plane * 4, 4), :, cols]
                remote(piece, piece, send_sem.at[sem + 1], recv_sem.at[sem], sibling).start()
        wait_bytes(dst.at[0:8], recv_sem.at[sem])
        wait_bytes(dst.at[0:8], send_sem.at[sem + 1])
        wait_bytes(dst.at[0:7], send_sem.at[sem])
        wait_bytes(dst.at[0, :, 0:7 * D_OWN], send_sem.at[sem])

    def norm_all(step, gain):
        def chunk(i, carry):
            g_buf[pl.ds(pl.multiple_of(i * TEAM_ROWS, TEAM_ROWS), TEAM_ROWS), :] = norm_rows(
                x_all[step, i].astype(F32), gain)
            return carry

        lax.fori_loop(0, TEAMS, chunk, 0)

    gather_team(hid_send, hid_land.at[slot], 0)
    wait_bytes(hid_land.at[0:TEAM - 1], recv_sem.at[0])
    for i in range(TEAM):
        x_team[ROWS * i:ROWS * (i + 1), :] = hid_land[i]

    for layer in range(LAYERS):
        base = 8 * layer
        h = norm_rows(x_team[...], norm_attn[layer:layer + 1, :])
        x_block = x_team[:, own_cols]
        loads[layer][0].wait()
        for c in range(Q_OWN // 256):
            cols = slice(c * 256, (c + 1) * 256)
            q = dot_f32(h, wq_buf[layer, :, cols])
            for i in range(TEAM):
                q_send[layer, i, :, cols] = q[ROWS * i:ROWS * (i + 1), :]
        for i in range(1, TEAM):
            to = lax.rem(slot + i, TEAM)
            remote(q_send.at[layer, to], q_land.at[layer, slot], send_sem.at[base + 1], recv_sem.at[base + 1],
                   mate(i)).start()
        for i in range(1, TEAM):
            to = lax.rem(slot + i, TEAM)
            remote(w_down.at[layer, :, pl.ds(pl.multiple_of(to * D_OWN, D_OWN), D_OWN)],
                   wd_buf.at[layer, pl.ds(pl.multiple_of(slot * F_OWN, 16), F_OWN)],
                   down_send.at[layer], down_recv.at[layer], mate(i)).start()
        q_land[layer, slot] = q_send[layer, slot]
        wait_bytes(q_land.at[layer, 0:TEAM - 1], recv_sem.at[base + 1])
        for pair, at, sender, col, width in q_segments():
            for r in range(ROWS):
                q_pairs[r, pair:pair + 1, at:at + width] = q_land[layer, sender, r:r + 1, col:col + width]

        loads[layer][1].wait()
        lane = lax.broadcasted_iota(jnp.int32, (16, WIDE), 1)
        key_pos = lax.broadcasted_iota(jnp.int32, (32, SEQ), 1)
        contexts = []
        for r in range(ROWS):
            q_even = jnp.where(lane < KV, q_pairs[r, :, 0:WIDE], 0.0).astype(BF16)
            q_odd = jnp.where(lane >= SHIFT, q_pairs[r, :, PAIR - WIDE:PAIR], 0.0).astype(BF16)
            scores = jnp.concatenate([dot_f32(q_even, kv_buf[layer, r, SHIFT:SHIFT + WIDE, :]),
                                      dot_f32(q_odd, kv_buf[layer, r, 0:WIDE, :])], axis=0) * QK_SCALE
            scores = jnp.where(key_pos < lengths[r], scores, -1e30)
            weights = jnp.exp(scores - jnp.max(scores, axis=-1, keepdims=True))
            probs = (weights / jnp.sum(weights, axis=-1, keepdims=True)).astype(BF16)
            contexts.append(dot_f32(probs, kv_buf[layer, r, SHIFT:SHIFT + LATENT, :], ((1,), (1,))).astype(BF16))
        o_send[layer] = dot_f32(pack[...], jnp.concatenate(contexts, axis=0)).astype(BF16)
        gather_team(o_send.at[layer], o_land.at[layer, slot], base + 2)
        o_land[layer, slot] = o_send[layer]
        wait_bytes(o_land.at[layer, 0:TEAM - 1], recv_sem.at[base + 2])

        o_heads[...] = dot_f32(spread[...], o_land[layer].reshape(TEAM * O_ROWS, LATENT)).astype(BF16)
        loads[layer][2].wait()

        def head(i, total):
            return total + dot_f32(o_heads[pl.ds(pl.multiple_of(i * TEAM_ROWS, TEAM_ROWS), TEAM_ROWS), :],
                                   wo_buf[layer, pl.ds(pl.multiple_of(i * LATENT, LATENT), LATENT), :])

        delta = lax.fori_loop(0, HEADS, head, jnp.zeros((TEAM_ROWS, D_OWN), F32))
        x_block = (x_block + delta).astype(BF16)
        if layer == 0:
            pl.semaphore_wait(entry_sem, TEAM - 1)
        gather_all(x_block, layer)

        norm_all(layer, norm_ffn[layer:layer + 1, :])
        loads[layer][3].wait()
        loads[layer][4].wait()
        gate_up = dot_f32(wgu_buf[layer], g_buf[...], ((1,), (1,)))
        act = (jax.nn.silu(gate_up[0:F_OWN]) * gate_up[F_OWN:]).astype(BF16)
        own_hidden = a_all.at[layer, pl.ds(pl.multiple_of(slot * F_OWN, 16), F_OWN)]
        own_hidden[...] = act
        gather_team(own_hidden, own_hidden, base + 3)
        wait_bytes(a_all.at[layer, 0:F_TEAM - F_OWN], recv_sem.at[base + 3])
        loads[layer][5].wait()
        wait_bytes(wd_buf.at[layer, 0:F_TEAM - F_OWN], down_recv.at[layer])
        part[layer] = dot_f32(a_all[layer], wd_buf[layer], ((0,), (0,))).reshape(TEAMS, TEAM_ROWS, D_OWN)

        def scatter(i, carry):
            to = lax.rem(team + i, TEAMS)
            remote(part.at[layer, to], land.at[layer, team], send_sem.at[base + 4], recv_sem.at[base + 4],
                   to * TEAM + slot).start()
            return carry

        lax.fori_loop(1, TEAMS, scatter, 0)
        land[layer, team] = part[layer, team]
        wait_bytes(land.at[layer, 0:TEAMS - 1], recv_sem.at[base + 4])
        total = land[layer, 0]
        for i in range(1, TEAMS):
            total = total + land[layer, i]
        x_block = (x_block.astype(F32) + total).astype(BF16)

        wait_bytes(q_land.at[layer, 0:TEAM - 1], send_sem.at[base + 1])
        wait_bytes(o_land.at[layer, 0:TEAM - 1], send_sem.at[base + 2])
        wait_bytes(a_all.at[layer, 0:F_TEAM - F_OWN], send_sem.at[base + 3])
        wait_bytes(land.at[layer, 0:TEAMS - 1], send_sem.at[base + 4])
        wait_bytes(wd_buf.at[layer, 0:F_TEAM - F_OWN], down_send.at[layer])
        if layer == 0:
            wait_bytes(hid_land.at[0:TEAM - 1], send_sem.at[0])
            own_block = xb_team.at[:, own_cols]
            own_block[...] = x_block
            gather_team(own_block, own_block, 5)
            wait_bytes(xb_team.at[:, 0:D - D_OWN], recv_sem.at[5])
            x_team[...] = xb_team[...].astype(F32)
            wait_bytes(xb_team.at[:, 0:D - D_OWN], send_sem.at[5])
        else:
            gather_all(x_block, LAYERS)

    norm_all(LAYERS, norm_final[...])
    out[...] = g_buf[...]


def make_selectors(pack, spread):
    row = lax.broadcasted_iota(jnp.int32, pack.shape, 0)
    col = lax.broadcasted_iota(jnp.int32, pack.shape, 1)
    seq = jnp.where(row >= HEADS, 1, 0)
    head = row - HEADS * seq
    hit = (col == seq * 32 + (head & 1) * 16 + (head >> 1)) & (row < ROWS * HEADS)
    pack[...] = jnp.where(hit, 1.0, 0.0).astype(BF16)
    shape = (TEAM_ROWS, TEAM * O_ROWS)
    row = lax.broadcasted_iota(jnp.int32, shape, 0)
    col = lax.broadcasted_iota(jnp.int32, shape, 1)
    head = col - (row >> 1) * O_ROWS - (row & 1) * HEADS
    for i in range(HEADS):
        spread[i * TEAM_ROWS:(i + 1) * TEAM_ROWS, :] = jnp.where(head == i, 1.0, 0.0).astype(BF16)


def decode(hidden, lengths, kv_cache, norm_attn, w_q, w_o, norm_ffn, w_gate, w_up, w_down, norm_final):
    vmem = pl.BlockSpec(memory_space=pltpu.VMEM)
    smem = pl.BlockSpec(memory_space=pltpu.SMEM)
    hbm = pl.BlockSpec(memory_space=pl.ANY)
    dma = pltpu.SemaphoreType.DMA
    return pl.pallas_call(
        decode_kernel,
        out_shape=jax.ShapeDtypeStruct((ALL_ROWS, D), BF16),
        in_specs=[vmem, smem, hbm, vmem, hbm, hbm, vmem, hbm, hbm, hbm, vmem],
        out_specs=vmem,
        scratch_shapes=[
            pltpu.VMEM((O_ROWS, 64), BF16),
            pltpu.VMEM((HEADS * TEAM_ROWS, TEAM * O_ROWS), BF16),
            pltpu.VMEM((ROWS, D), F32),
            pltpu.VMEM((TEAM, ROWS, D), F32),
            pltpu.VMEM((TEAM_ROWS, D), F32),
            pltpu.VMEM((TEAM_ROWS, D), BF16),
            pltpu.VMEM((LAYERS, D, Q_OWN), BF16),
            pltpu.VMEM((LAYERS, ROWS, KV + 2 * SHIFT, SEQ), BF16),
            pltpu.VMEM((LAYERS, HEADS * LATENT, D_OWN), BF16),
            pltpu.VMEM((LAYERS, 2 * F_OWN, D), BF16),
            pltpu.VMEM((LAYERS, F_TEAM, D_OWN), BF16),
            pltpu.VMEM((LAYERS, TEAM, ROWS, Q_OWN), F32),
            pltpu.VMEM((LAYERS, TEAM, ROWS, Q_OWN), F32),
            pltpu.VMEM((ROWS, 16, PAIR), F32),
            pltpu.VMEM((LAYERS, O_ROWS, LATENT), BF16),
            pltpu.VMEM((LAYERS, TEAM, O_ROWS, LATENT), BF16),
            pltpu.VMEM((HEADS * TEAM_ROWS, LATENT), BF16),
            pltpu.VMEM((LAYERS + 1, TEAMS, TEAM_ROWS, D), BF16),
            pltpu.VMEM((ALL_ROWS, D), BF16),
            pltpu.VMEM((LAYERS, F_TEAM, ALL_ROWS), BF16),
            pltpu.VMEM((LAYERS, TEAMS, TEAM_ROWS, D_OWN), F32),
            pltpu.VMEM((LAYERS, TEAMS, TEAM_ROWS, D_OWN), F32),
            dma((LAYERS, 6)),
            pltpu.SemaphoreType.REGULAR,
            dma((22,)),
            dma((22,)),
            dma((LAYERS + 1, 4)),
            dma((LAYERS,)),
            dma((LAYERS,)),
        ],
        compiler_params=pltpu.CompilerParams(collective_id=0, has_side_effects=True, vmem_limit_bytes=60 * 1024 * 1024),
        name='decode',
    )(hidden, lengths, kv_cache, norm_attn, w_q, w_o, norm_ffn, w_gate, w_up, w_down, norm_final)


def solution(mesh):
    row_axes = ('rep', 'dp')
    specs_in = (P(row_axes, None), P(row_axes), P(None, row_axes, None, None), P(), P(), P(), P(),
                P(None, None, 'dp'), P(None, None, 'dp'), P(None, 'dp', None), P(), P(None, 'dp'))

    def device_step(hidden, lengths, kv_cache, norm_attn, w_q, w_o, norm_ffn, w_gate, w_up, w_down, norm_final, w_head):
        normed = decode(hidden, lengths, jnp.swapaxes(kv_cache, 2, 3), norm_attn, w_q, w_o, norm_ffn,
                        jnp.swapaxes(w_gate, 1, 2), jnp.swapaxes(w_up, 1, 2), w_down, norm_final.reshape(1, -1))
        return jnp.dot(normed, w_head, preferred_element_type=jnp.float32)

    return jax.shard_map(device_step, mesh=mesh, in_specs=specs_in, out_specs=P('rep', 'dp'), check_vma=False)
```

time: 609 us -> 124 us (0.20)
  waiting for transfers between devices: 491 us -> 0 us
  Pallas kernels: 0 us -> 119 us
  matrix products: 83.6 us -> 5.28 us
  local copies, waits for them, and re-layouts: 13.9 us -> 0 us
  between operations: 13.3 us -> 0.01 us
    unnamed x7 -> x0, waiting for transfers between devices: 298 us -> none
    all_gather x3 -> x0, waiting for transfers between devices: 193 us -> none  [device_step(): gathered = lax.all_gather(normed, 'dp', axis=0, tiled=True)]
    pallas_call x0 -> x1, Pallas kernels: none -> 119 us  [decode(): pl.pallas_call(decode_kernel, out_shape=jax.ShapeDtypeStruct((ALL_ROWS, D...]
    dot_general x13 -> x1, matrix products: 83.6 us -> 5.28 us  [device_step(): return jnp.dot(normed, w_head, preferred_element_type=jnp.float32)]
    unnamed x29 -> x0, local copies, waits for them, and re-layouts: 6.56 us -> none
  transfers between devices with their start and end apart: 5 -> 0, of which waited for: 5 -> 0; matrix products, arithmetic and copies ran while one was open for 0% -> 0% of each run, Pallas kernels for 0% -> 0%
where the time goes in v2:
time: 124 us
  Pallas kernels  119 us (96%)
  matrix products  5.28 us (4%)
    pallas_call x1, Pallas kernels, decode(): pl.pallas_call(decode_kernel, out_shape=jax.ShapeDtypeStruct((ALL_ROWS, D...  119 us
    dot_general x1, matrix products, device_step(): return jnp.dot(normed, w_head, preferred_element_type=jnp.float32)  5.28 us

profile of v2, /device:TPU:1, one launch (start us, length us, event | category | flops | bytes accessed | tf_op | source)
XLA Modules:
  0.0 123.8 jit_solution(12676267917067395100)
XLA Ops:
  0.0 118.5 %decode.1 = bf16[256,2048]{1,0:T(8,128)(2,1)} custom-call(bf16[2,2048]{1,0:T(2,128)(2,1)} %hidden.1, s32[2]{0:T(128)} %lengths.1, bf16[2,2,576,512]{3,2,1,0:T(8,128)(2,1)} %bitcast.6, f32[2,2048]{1,0:T(2,128)} %norm_attn.1, bf16[2,2048,11520]{2,1,0:T(8,128)(2,1)} %w_q.1, bf16[2,10240,2048]{2,1,0:T(8,128)(2,1)} %w_o.1, f32[2,2048]{1,0:T(2,128)} %norm_ffn.1, ...), custom_call_target="tpu_custom_call" | custom-call | tf_op jit(solution)/shard_map/decode/pallas_call | solution.py:289
  118.5 5.3 %fusion = f32[256,1210]{0,1:T(8,128)} fusion(bf16[256,2048]{1,0:T(8,128)(2,1)} %decode.1, bf16[2048,1210]{0,1:T(8,128)(2,1)} %param.23), kind=kOutput, calls=%fused_computation | convolution fusion | flops 1268776960 | bytes 7243776 | tf_op jit(solution)/shard_map/dot_general | solution.py:338

commit v3 on v2

v3 whole, which is shorter than its diff:
```python
import jax
import jax.numpy as jnp
from jax import lax
from jax.experimental import pallas as pl
from jax.experimental.pallas import tpu as pltpu
from jax.sharding import PartitionSpec as P

MESH = pl.DeviceIdType.MESH
QK_SCALE = 192 ** -0.5
NORM_EPS = 1e-6

LAYERS = 2
ROWS = 2
TEAM = 8
TEAMS = 16
TEAM_ROWS = ROWS * TEAM
ALL_ROWS = TEAM_ROWS * TEAMS
D = 2048
D_OWN = D // TEAM
HEADS = 20
LATENT = 512
KV = 576
SEQ = 512
Q_COLS = HEADS * KV
Q_OWN = 1536
Q_LAST = Q_COLS - Q_OWN
PAIR = 2 * KV
PAIRS = HEADS // 2
SHIFT = 64
WIDE = KV + SHIFT
O_ROWS = 24
F_OWN = 80
F_TEAM = F_OWN * TEAM
VOCAB_OWN = 1210
HEAD_CHUNK = 304
F32 = jnp.float32
BF16 = jnp.bfloat16


def norm_rows(x, gain):
    inv_rms = lax.rsqrt(jnp.mean(x * x, axis=-1, keepdims=True) + NORM_EPS)
    return (x * inv_rms * gain).astype(BF16)


def dot_f32(a, b, contract=((1,), (0,))):
    return lax.dot_general(a, b, (contract, ((), ())), preferred_element_type=F32)


def wait_bytes(ref, sem):
    pltpu.make_async_copy(ref, ref, sem).wait()


def q_segments():
    pieces = []
    for pair in range(PAIRS):
        at, end = pair * PAIR, (pair + 1) * PAIR
        while at < end:
            sender = at // Q_OWN
            first = min(sender * Q_OWN, Q_LAST)
            stop = min(end, (sender + 1) * Q_OWN, Q_COLS)
            pieces.append((pair, at - pair * PAIR, sender, at - first, stop - at))
            at = stop
    return pieces


def decode_kernel(hidden, lengths, kv_cache, norm_attn, w_q, w_o, norm_ffn, w_gate, w_up, w_down, norm_final, w_head,
                  out, head_buf, logits, pack, spread, hid_send, hid_land, x_team, xb_team, wq_buf, kv_buf, wo_buf, wgu_buf, wd_buf,
                  q_send, q_land, q_pairs, o_send, o_land, o_heads, x_all, g_buf, a_all, part, land,
                  load_sem, entry_sem, send_sem, recv_sem, plane_sem, down_send, down_recv, head_sem, out_sem):
    me = lax.axis_index('dp')
    team, slot = me // TEAM, lax.rem(me, TEAM)
    plane, core = team // 4, lax.rem(me, 2)
    sibling = me + 1 - 2 * core
    own_cols = pl.ds(pl.multiple_of(slot * D_OWN, D_OWN), D_OWN)
    q_start = pl.multiple_of(jnp.minimum(slot * Q_OWN, Q_LAST), 128)

    pending = []

    def take(layer, i):
        loads[layer][i].wait()

    def mate(i):
        return team * TEAM + lax.rem(slot + i, TEAM)

    def remote(src, dst, ssem, rsem, device):
        return pltpu.make_async_remote_copy(src, dst, ssem, rsem, device_id={'dp': device}, device_id_type=MESH)

    barrier = pltpu.get_barrier_semaphore()
    for i in range(1, TEAM):
        pl.semaphore_signal(barrier, inc=1, device_id={'dp': mate(i)}, device_id_type=MESH)

    def greet(i, carry):
        pl.semaphore_signal(barrier, inc=1, device_id={'dp': lax.rem(me + i * TEAM, TEAM * TEAMS)}, device_id_type=MESH)
        return carry

    lax.fori_loop(1, TEAMS, greet, 0)

    loads = []
    for layer in range(LAYERS):
        batch = [
            (w_q.at[layer, :, pl.ds(q_start, Q_OWN)], wq_buf.at[layer]),
            (kv_cache.at[layer], kv_buf.at[layer, :, pl.ds(SHIFT, KV)]),
            (w_o.at[layer, :, own_cols], wo_buf.at[layer]),
            (w_gate.at[layer], wgu_buf.at[layer, pl.ds(0, F_OWN)]),
            (w_up.at[layer], wgu_buf.at[layer, pl.ds(F_OWN, F_OWN)]),
            (w_down.at[layer, :, own_cols], wd_buf.at[layer, pl.ds(pl.multiple_of(slot * F_OWN, 16), F_OWN)]),
        ]
        loads.append([pltpu.make_async_copy(src, dst, load_sem.at[layer, i]) for i, (src, dst) in enumerate(batch)])
    for batch in loads:
        for copy in batch:
            copy.start()
    head_load = pltpu.make_async_copy(w_head, head_buf, head_sem)
    head_load.start()

    for layer in range(LAYERS):
        for r in range(ROWS):
            kv_buf[layer, r, 0:SHIFT, :] = jnp.zeros((SHIFT, SEQ), BF16)
            kv_buf[layer, r, SHIFT + KV:, :] = jnp.zeros((SHIFT, SEQ), BF16)
    q_pairs[...] = jnp.zeros_like(q_pairs)
    make_selectors(pack, spread)
    hid_send[...] = hidden[...].astype(F32)
    hid_land[slot] = hid_send[...]

    pl.semaphore_wait(barrier, TEAM - 1 + TEAMS - 1)
    for i in range(1, TEAM):
        pl.semaphore_signal(entry_sem, inc=1, device_id={'dp': mate(i)}, device_id_type=MESH)

    def gather_team(src, dst, sem):
        for i in range(1, TEAM):
            remote(src, dst, send_sem.at[sem], recv_sem.at[sem], mate(i)).start()
            pending.append((src, send_sem.at[sem]))

    def share_down(layer):
        for i in range(1, TEAM):
            to = lax.rem(slot + i, TEAM)
            remote(w_down.at[layer, :, pl.ds(pl.multiple_of(to * D_OWN, D_OWN), D_OWN)],
                   wd_buf.at[layer, pl.ds(pl.multiple_of(slot * F_OWN, 16), F_OWN)],
                   down_send.at[layer], down_recv.at[layer], mate(i)).start()
        pending.append((wd_buf.at[layer, 0:F_TEAM - F_OWN], down_send.at[layer]))

    def gather_all(block, step, gain):
        dst = x_all.at[step]
        mine = dst.at[team, :, own_cols]
        mine[...] = block
        direct, passed = send_sem.at[16 + 2 * step], send_sem.at[17 + 2 * step]
        planes = (plane, plane + 1 - 2 * lax.rem(plane, 2), 3 - plane, lax.rem(plane + 2, 4))
        for k in (3, 2, 1, 0):

            def send(i, carry, k=k):
                spot = lax.rem(lax.rem(me, 32) // 2 + 24 - i, 16)
                remote(mine, mine, direct, plane_sem.at[step, k], planes[k] * 32 + spot * 2 + core).start()
                return carry

            def send_near(i, carry, k=k):
                spot = lax.rem(lax.rem(me, 32) // 2 + i, 16)
                remote(mine, mine, direct, plane_sem.at[step, k], planes[k] * 32 + spot * 2 + core).start()
                return carry

            if k:
                lax.fori_loop(0, 16, send, 0)
            else:
                lax.fori_loop(1, 16, send_near, 0)
        pending.append((dst.at[0:7], direct))
        pending.append((dst.at[0, :, 0:7 * D_OWN], direct))
        pending.append((dst.at[0:8], passed))

        def finish(k):
            wait_bytes(dst.at[0:4, :, 0:4 * D_OWN], plane_sem.at[step, 4 + k])

            def chunk(i, carry):
                row = planes[k] * 4 + i
                g_buf[pl.ds(pl.multiple_of(row * TEAM_ROWS, TEAM_ROWS), TEAM_ROWS), :] = norm_rows(
                    dst[row].astype(F32), gain)
                return carry

            lax.fori_loop(0, 4, chunk, 0)

        for k in range(4):
            if k == 0:
                wait_bytes(dst.at[0:3, :, 0:5 * D_OWN], plane_sem.at[step, k])
            else:
                wait_bytes(dst.at[0:4, :, 0:4 * D_OWN], plane_sem.at[step, k])
            for x in range(4):
                cols = pl.ds(pl.multiple_of((2 * x + core) * D_OWN, D_OWN), D_OWN)
                piece = dst.at[pl.ds(planes[k] * 4, 4), :, cols]
                remote(piece, piece, passed, plane_sem.at[step, 4 + k], sibling).start()
            if k:
                finish(k - 1)
        finish(3)

    gather_team(hid_send, hid_land.at[slot], 0)
    share_down(0)
    wait_bytes(hid_land.at[0:TEAM - 1], recv_sem.at[0])
    for i in range(TEAM):
        x_team[ROWS * i:ROWS * (i + 1), :] = hid_land[i]

    for layer in range(LAYERS):
        base = 8 * layer
        h = norm_rows(x_team[...], norm_attn[layer:layer + 1, :])
        x_block = x_team[:, own_cols]
        take(layer, 0)
        for c in range(Q_OWN // 256):
            cols = slice(c * 256, (c + 1) * 256)
            q = dot_f32(h, wq_buf[layer, :, cols])
            for i in range(TEAM):
                q_send[layer, i, :, cols] = q[ROWS * i:ROWS * (i + 1), :]
        for i in range(1, TEAM):
            to = lax.rem(slot + i, TEAM)
            remote(q_send.at[layer, to], q_land.at[layer, slot], send_sem.at[base + 1], recv_sem.at[base + 1],
                   mate(i)).start()
        pending.append((q_land.at[layer, 0:TEAM - 1], send_sem.at[base + 1]))
        q_land[layer, slot] = q_send[layer, slot]
        wait_bytes(q_land.at[layer, 0:TEAM - 1], recv_sem.at[base + 1])
        for pair, at, sender, col, width in q_segments():
            for r in range(ROWS):
                q_pairs[r, pair:pair + 1, at:at + width] = q_land[layer, sender, r:r + 1, col:col + width]

        take(layer, 1)
        lane = lax.broadcasted_iota(jnp.int32, (16, WIDE), 1)
        key_pos = lax.broadcasted_iota(jnp.int32, (32, SEQ), 1)
        for r in range(ROWS):
            q_even = jnp.where(lane < KV, q_pairs[r, :, 0:WIDE], 0.0).astype(BF16)
            q_odd = jnp.where(lane >= SHIFT, q_pairs[r, :, PAIR - WIDE:PAIR], 0.0).astype(BF16)
            scores = jnp.concatenate([dot_f32(q_even, kv_buf[layer, r, SHIFT:SHIFT + WIDE, :]),
                                      dot_f32(q_odd, kv_buf[layer, r, 0:WIDE, :])], axis=0) * QK_SCALE
            scores = jnp.where(key_pos < lengths[r], scores, -1e30)
            weights = jnp.exp(scores - jnp.max(scores, axis=-1, keepdims=True))
            probs = (weights / jnp.sum(weights, axis=-1, keepdims=True)).astype(BF16)
            context = dot_f32(probs, kv_buf[layer, r, SHIFT:SHIFT + LATENT, :], ((1,), (1,))).astype(BF16)
            o_send[layer, r] = dot_f32(pack[...], context).astype(BF16)
            gather_team(o_send.at[layer, r], o_land.at[layer, slot, r], base + 2)
            o_land[layer, slot, r] = o_send[layer, r]
        wait_bytes(o_land.at[layer, 0:TEAM - 1], recv_sem.at[base + 2])

        o_heads[...] = dot_f32(spread[...], o_land[layer].reshape(TEAM_ROWS * O_ROWS, LATENT)).astype(BF16)
        take(layer, 2)

        heads = jnp.concatenate([o_heads[i * TEAM_ROWS:(i + 1) * TEAM_ROWS, :] for i in range(HEADS)], axis=1)
        delta = dot_f32(heads, wo_buf[layer])
        x_block = (x_block + delta).astype(BF16)
        if layer == 0:
            pl.semaphore_wait(entry_sem, TEAM - 1)
        gather_all(x_block, layer, norm_ffn[layer:layer + 1, :])

        take(layer, 3)
        take(layer, 4)
        gate_up = dot_f32(wgu_buf[layer], g_buf[...], ((1,), (1,)))
        act = (jax.nn.silu(gate_up[0:F_OWN]) * gate_up[F_OWN:]).astype(BF16)
        own_hidden = a_all.at[layer, pl.ds(pl.multiple_of(slot * F_OWN, 16), F_OWN)]
        own_hidden[...] = act
        gather_team(own_hidden, own_hidden, base + 3)
        wait_bytes(a_all.at[layer, 0:F_TEAM - F_OWN], recv_sem.at[base + 3])
        take(layer, 5)
        wait_bytes(wd_buf.at[layer, 0:F_TEAM - F_OWN], down_recv.at[layer])
        part[layer] = dot_f32(a_all[layer], wd_buf[layer], ((0,), (0,))).reshape(TEAMS, TEAM_ROWS, D_OWN)

        def scatter(i, carry):
            to = lax.rem(team + i, TEAMS)
            remote(part.at[layer, to], land.at[layer, team], send_sem.at[base + 4], recv_sem.at[base + 4],
                   to * TEAM + slot).start()
            return carry

        lax.fori_loop(1, TEAMS, scatter, 0)
        pending.append((land.at[layer, 0:TEAMS - 1], send_sem.at[base + 4]))
        if layer + 1 < LAYERS:
            share_down(layer + 1)
        land[layer, team] = part[layer, team]
        wait_bytes(land.at[layer, 0:TEAMS - 1], recv_sem.at[base + 4])
        total = land[layer, 0]
        for i in range(1, TEAMS):
            total = total + land[layer, i]
        x_block = (x_block.astype(F32) + total).astype(BF16)

        if layer == 0:
            own_block = xb_team.at[:, own_cols]
            own_block[...] = x_block
            gather_team(own_block, own_block, 5)
            wait_bytes(xb_team.at[:, 0:D - D_OWN], recv_sem.at[5])
            x_team[...] = xb_team[...].astype(F32)
        else:
            gather_all(x_block, LAYERS, norm_final[...])

    head_load.wait()
    copies = []
    for i, first in enumerate(range(0, VOCAB_OWN, HEAD_CHUNK)):
        size = min(HEAD_CHUNK, VOCAB_OWN - first)
        logits[first:first + size, :] = dot_f32(head_buf[first:first + size, :], g_buf[...], ((1,), (1,)))
        copies.append(pltpu.make_async_copy(logits.at[first:first + size], out.at[first:first + size], out_sem.at[i]))
        copies[-1].start()
    for copy in copies:
        copy.wait()
    for ref, sem in pending:
        wait_bytes(ref, sem)


def make_selectors(pack, spread):
    row = lax.broadcasted_iota(jnp.int32, pack.shape, 0)
    col = lax.broadcasted_iota(jnp.int32, pack.shape, 1)
    hit = (col == (row & 1) * 16 + (row >> 1)) & (row < HEADS)
    pack[...] = jnp.where(hit, 1.0, 0.0).astype(BF16)
    shape = (TEAM_ROWS, TEAM_ROWS * O_ROWS)
    row = lax.broadcasted_iota(jnp.int32, shape, 0)
    col = lax.broadcasted_iota(jnp.int32, shape, 1)
    head = col - row * O_ROWS
    for i in range(HEADS):
        spread[i * TEAM_ROWS:(i + 1) * TEAM_ROWS, :] = jnp.where(head == i, 1.0, 0.0).astype(BF16)


def decode(hidden, lengths, kv_cache, norm_attn, w_q, w_o, norm_ffn, w_gate, w_up, w_down, norm_final, w_head):
    vmem = pl.BlockSpec(memory_space=pltpu.VMEM)
    smem = pl.BlockSpec(memory_space=pltpu.SMEM)
    hbm = pl.BlockSpec(memory_space=pl.ANY)
    dma = pltpu.SemaphoreType.DMA
    return pl.pallas_call(
        decode_kernel,
        out_shape=jax.ShapeDtypeStruct((VOCAB_OWN, ALL_ROWS), F32),
        in_specs=[vmem, smem, hbm, vmem, hbm, hbm, vmem, hbm, hbm, hbm, vmem, hbm],
        out_specs=hbm,
        scratch_shapes=[
            pltpu.VMEM((VOCAB_OWN, D), BF16),
            pltpu.VMEM((VOCAB_OWN, ALL_ROWS), F32),
            pltpu.VMEM((O_ROWS, 32), BF16),
            pltpu.VMEM((HEADS * TEAM_ROWS, TEAM_ROWS * O_ROWS), BF16),
            pltpu.VMEM((ROWS, D), F32),
            pltpu.VMEM((TEAM, ROWS, D), F32),
            pltpu.VMEM((TEAM_ROWS, D), F32),
            pltpu.VMEM((TEAM_ROWS, D), BF16),
            pltpu.VMEM((LAYERS, D, Q_OWN), BF16),
            pltpu.VMEM((LAYERS, ROWS, KV + 2 * SHIFT, SEQ), BF16),
            pltpu.VMEM((LAYERS, HEADS * LATENT, D_OWN), BF16),
            pltpu.VMEM((LAYERS, 2 * F_OWN, D), BF16),
            pltpu.VMEM((LAYERS, F_TEAM, D_OWN), BF16),
            pltpu.VMEM((LAYERS, TEAM, ROWS, Q_OWN), F32),
            pltpu.VMEM((LAYERS, TEAM, ROWS, Q_OWN), F32),
            pltpu.VMEM((ROWS, 16, PAIR), F32),
            pltpu.VMEM((LAYERS, ROWS, O_ROWS, LATENT), BF16),
            pltpu.VMEM((LAYERS, TEAM, ROWS, O_ROWS, LATENT), BF16),
            pltpu.VMEM((HEADS * TEAM_ROWS, LATENT), BF16),
            pltpu.VMEM((LAYERS + 1, TEAMS, TEAM_ROWS, D), BF16),
            pltpu.VMEM((ALL_ROWS, D), BF16),
            pltpu.VMEM((LAYERS, F_TEAM, ALL_ROWS), BF16),
            pltpu.VMEM((LAYERS, TEAMS, TEAM_ROWS, D_OWN), F32),
            pltpu.VMEM((LAYERS, TEAMS, TEAM_ROWS, D_OWN), F32),
            dma((LAYERS, 6)),
            pltpu.SemaphoreType.REGULAR,
            dma((22,)),
            dma((22,)),
            dma((LAYERS + 1, 8)),
            dma((LAYERS,)),
            dma((LAYERS,)),
            dma,
            dma((-(-VOCAB_OWN // HEAD_CHUNK),)),
        ],
        compiler_params=pltpu.CompilerParams(collective_id=0, has_side_effects=True, vmem_limit_bytes=60 * 1024 * 1024),
        name='decode',
    )(hidden, lengths, kv_cache, norm_attn, w_q, w_o, norm_ffn, w_gate, w_up, w_down, norm_final, w_head)


def solution(mesh):
    row_axes = ('rep', 'dp')
    specs_in = (P(row_axes, None), P(row_axes), P(None, row_axes, None, None), P(), P(), P(), P(),
                P(None, None, 'dp'), P(None, None, 'dp'), P(None, 'dp', None), P(), P(None, 'dp'))

    def device_step(hidden, lengths, kv_cache, norm_attn, w_q, w_o, norm_ffn, w_gate, w_up, w_down, norm_final, w_head):
        logits = decode(hidden, lengths, jnp.swapaxes(kv_cache, 2, 3), norm_attn, w_q, w_o, norm_ffn,
                        jnp.swapaxes(w_gate, 1, 2), jnp.swapaxes(w_up, 1, 2), w_down, norm_final.reshape(1, -1),
                        jnp.swapaxes(w_head, 0, 1))
        return jnp.swapaxes(logits, 0, 1)

    return jax.shard_map(device_step, mesh=mesh, in_specs=specs_in, out_specs=P('rep', 'dp'), check_vma=False)
```

time: 124 us -> 115 us (0.927)
  Pallas kernels: 119 us -> 112 us
  matrix products: 5.28 us -> 0 us
  local copies, waits for them, and re-layouts: 0 us -> 2.41 us
    pallas_call x1, Pallas kernels: 119 us -> 112 us  [decode(): pl.pallas_call(decode_kernel, out_shape=jax.ShapeDtypeStruct((VOCAB_OWN,...]
    dot_general x1 -> x0, matrix products: 5.28 us -> none  [device_step(): return jnp.dot(normed, w_head, preferred_element_type=jnp.float32)]
    unnamed x0 -> x1, local copies, waits for them, and re-layouts: none -> 2.41 us
where the time goes in v3:
time: 115 us
  Pallas kernels  112 us (97%)
  local copies, waits for them, and re-layouts  2.41 us (2%)
    pallas_call x1, Pallas kernels, decode(): pl.pallas_call(decode_kernel, out_shape=jax.ShapeDtypeStruct((VOCAB_OWN,...  112 us
    unnamed x1, local copies, waits for them, and re-layouts  2.41 us

profile of v3, /device:TPU:1, one launch (start us, length us, event | category | flops | bytes accessed | tf_op | source)
XLA Modules:
  0.0 114.8 jit_solution(12336109814709017316)
XLA Ops:
  0.0 112.4 %decode.1 = f32[1210,256]{1,0:T(8,128)} custom-call(bf16[2,2048]{1,0:T(2,128)(2,1)} %hidden.1, s32[2]{0:T(128)} %lengths.1, bf16[2,2,576,512]{3,2,1,0:T(8,128)(2,1)} %bitcast.8, f32[2,2048]{1,0:T(2,128)} %norm_attn.1, bf16[2,2048,11520]{2,1,0:T(8,128)(2,1)} %w_q.1, bf16[2,10240,2048]{2,1,0:T(8,128)(2,1)} %w_o.1, f32[2,2048]{1,0:T(2,128)} %norm_ffn.1, ...), custom_call_target="tpu_custom_call" | custom-call | tf_op jit(solution)/shard_map/decode/pallas_call | solution.py:314
  112.4 2.4 %copy.14 = f32[256,1210]{0,1:T(8,128)} copy(f32[256,1210]{0,1:T(8,128)} %bitcast.6) | data formatting | bytes 2478080

commit v4 on v3

--- a/solution.py
+++ b/solution.py
@@ -15,6 +15,7 @@
 TEAMS = 16
 TEAM_ROWS = ROWS * TEAM
 ALL_ROWS = TEAM_ROWS * TEAMS
+HALF = ALL_ROWS // 2
 D = 2048
 D_OWN = D // TEAM
 HEADS = 20
@@ -64,9 +65,9 @@
 
 
 def decode_kernel(hidden, lengths, kv_cache, norm_attn, w_q, w_o, norm_ffn, w_gate, w_up, w_down, norm_final, w_head,
-                  out, head_buf, logits, pack, spread, hid_send, hid_land, x_team, xb_team, wq_buf, kv_buf, wo_buf, wgu_buf, wd_buf,
+                  out, head_buf, logits, pack, spread, hid_land, x_team, xb_team, wq_buf, kv_buf, wo_buf, wgu_buf, wd_buf,
                   q_send, q_land, q_pairs, o_send, o_land, o_heads, x_all, g_buf, a_all, part, land,
-                  load_sem, entry_sem, send_sem, recv_sem, plane_sem, down_send, down_recv, head_sem, out_sem):
+                  load_sem, entry_sem, send_sem, recv_sem, plane_sem, down_send, down_recv, near_sem, head_sem, out_sem):
     me = lax.axis_index('dp')
     team, slot = me // TEAM, lax.rem(me, TEAM)
     plane, core = team // 4, lax.rem(me, 2)
@@ -118,8 +119,7 @@
             kv_buf[layer, r, SHIFT + KV:, :] = jnp.zeros((SHIFT, SEQ), BF16)
     q_pairs[...] = jnp.zeros_like(q_pairs)
     make_selectors(pack, spread)
-    hid_send[...] = hidden[...].astype(F32)
-    hid_land[slot] = hid_send[...]
+    hid_land[slot] = hidden[...]
 
     pl.semaphore_wait(barrier, TEAM - 1 + TEAMS - 1)
     for i in range(1, TEAM):
@@ -138,7 +138,7 @@
                    down_send.at[layer], down_recv.at[layer], mate(i)).start()
         pending.append((wd_buf.at[layer, 0:F_TEAM - F_OWN], down_send.at[layer]))
 
-    def gather_all(block, step, gain):
+    def gather_all(block, step, gain, use_half):
         dst = x_all.at[step]
         mine = dst.at[team, :, own_cols]
         mine[...] = block
@@ -175,24 +175,25 @@
 
             lax.fori_loop(0, 4, chunk, 0)
 
-        for k in range(4):
-            if k == 0:
-                wait_bytes(dst.at[0:3, :, 0:5 * D_OWN], plane_sem.at[step, k])
-            else:
-                wait_bytes(dst.at[0:4, :, 0:4 * D_OWN], plane_sem.at[step, k])
-            for x in range(4):
-                cols = pl.ds(pl.multiple_of((2 * x + core) * D_OWN, D_OWN), D_OWN)
-                piece = dst.at[pl.ds(planes[k] * 4, 4), :, cols]
-                remote(piece, piece, passed, plane_sem.at[step, 4 + k], sibling).start()
-            if k:
-                finish(k - 1)
-        finish(3)
-
-    gather_team(hid_send, hid_land.at[slot], 0)
+        for half in range(2):
+            for k in (2 * half, 2 * half + 1):
+                if k == 0:
+                    wait_bytes(dst.at[0:3, :, 0:5 * D_OWN], plane_sem.at[step, k])
+                else:
+                    wait_bytes(dst.at[0:4, :, 0:4 * D_OWN], plane_sem.at[step, k])
+                for x in range(4):
+                    cols = pl.ds(pl.multiple_of((2 * x + core) * D_OWN, D_OWN), D_OWN)
+                    piece = dst.at[pl.ds(planes[k] * 4, 4), :, cols]
+                    remote(piece, piece, passed, plane_sem.at[step, 4 + k], sibling).start()
+            finish(2 * half)
+            finish(2 * half + 1)
+            use_half(half)
+
+    gather_team(hidden, hid_land.at[slot], 0)
     share_down(0)
     wait_bytes(hid_land.at[0:TEAM - 1], recv_sem.at[0])
     for i in range(TEAM):
-        x_team[ROWS * i:ROWS * (i + 1), :] = hid_land[i]
+        x_team[ROWS * i:ROWS * (i + 1), :] = hid_land[i].astype(F32)
 
     for layer in range(LAYERS):
         base = 8 * layer
@@ -203,7 +204,7 @@
             cols = slice(c * 256, (c + 1) * 256)
             q = dot_f32(h, wq_buf[layer, :, cols])
             for i in range(TEAM):
-                q_send[layer, i, :, cols] = q[ROWS * i:ROWS * (i + 1), :]
+                q_send[layer, i, :, cols] = q[ROWS * i:ROWS * (i + 1), :].astype(BF16)
         for i in range(1, TEAM):
             to = lax.rem(slot + i, TEAM)
             remote(q_send.at[layer, to], q_land.at[layer, slot], send_sem.at[base + 1], recv_sem.at[base + 1],
@@ -212,8 +213,9 @@
         q_land[layer, slot] = q_send[layer, slot]
         wait_bytes(q_land.at[layer, 0:TEAM - 1], recv_sem.at[base + 1])
         for pair, at, sender, col, width in q_segments():
+            piece = q_land[layer, sender, :, col:col + width].astype(F32)
             for r in range(ROWS):
-                q_pairs[r, pair:pair + 1, at:at + width] = q_land[layer, sender, r:r + 1, col:col + width]
+                q_pairs[r, pair:pair + 1, at:at + width] = piece[r:r + 1]
 
         take(layer, 1)
         lane = lax.broadcasted_iota(jnp.int32, (16, WIDE), 1)
@@ -228,9 +230,21 @@
             probs = (weights / jnp.sum(weights, axis=-1, keepdims=True)).astype(BF16)
             context = dot_f32(probs, kv_buf[layer, r, SHIFT:SHIFT + LATENT, :], ((1,), (1,))).astype(BF16)
             o_send[layer, r] = dot_f32(pack[...], context).astype(BF16)
-            gather_team(o_send.at[layer, r], o_land.at[layer, slot, r], base + 2)
+            block, dst = o_send.at[layer, r], o_land.at[layer, slot, r]
+            osem, orecv = send_sem.at[base + 2], recv_sem.at[base + 2]
+            for i in (4, 4 + 1 - 2 * core):
+                remote(block, dst, osem, orecv, mate(i)).start()
+            remote(block, dst, osem, near_sem.at[layer, r, 0], mate(2)).start()
+            remote(block, dst, osem, near_sem.at[layer, r, 1], mate(TEAM - 2)).start()
+            remote(block, dst, osem, orecv, sibling).start()
             o_land[layer, slot, r] = o_send[layer, r]
-        wait_bytes(o_land.at[layer, 0:TEAM - 1], recv_sem.at[base + 2])
+            pending.extend([(block, osem)] * (TEAM - 1))
+        for r in range(ROWS):
+            for side, i in enumerate((TEAM - 2, 2)):
+                piece = o_land.at[layer, lax.rem(slot + i, TEAM), r]
+                wait_bytes(piece, near_sem.at[layer, r, side])
+                remote(piece, piece, send_sem.at[base + 2], recv_sem.at[base + 2], sibling).start()
+        wait_bytes(o_land.at[layer, 0:TEAM - 3], recv_sem.at[base + 2])
 
         o_heads[...] = dot_f32(spread[...], o_land[layer].reshape(TEAM_ROWS * O_ROWS, LATENT)).astype(BF16)
         take(layer, 2)
@@ -240,27 +254,39 @@
         x_block = (x_block + delta).astype(BF16)
         if layer == 0:
             pl.semaphore_wait(entry_sem, TEAM - 1)
-        gather_all(x_block, layer, norm_ffn[layer:layer + 1, :])
-
-        take(layer, 3)
-        take(layer, 4)
-        gate_up = dot_f32(wgu_buf[layer], g_buf[...], ((1,), (1,)))
-        act = (jax.nn.silu(gate_up[0:F_OWN]) * gate_up[F_OWN:]).astype(BF16)
-        own_hidden = a_all.at[layer, pl.ds(pl.multiple_of(slot * F_OWN, 16), F_OWN)]
-        own_hidden[...] = act
-        gather_team(own_hidden, own_hidden, base + 3)
-        wait_bytes(a_all.at[layer, 0:F_TEAM - F_OWN], recv_sem.at[base + 3])
-        take(layer, 5)
-        wait_bytes(wd_buf.at[layer, 0:F_TEAM - F_OWN], down_recv.at[layer])
-        part[layer] = dot_f32(a_all[layer], wd_buf[layer], ((0,), (0,))).reshape(TEAMS, TEAM_ROWS, D_OWN)
-
-        def scatter(i, carry):
-            to = lax.rem(team + i, TEAMS)
-            remote(part.at[layer, to], land.at[layer, team], send_sem.at[base + 4], recv_sem.at[base + 4],
-                   to * TEAM + slot).start()
-            return carry
-
-        lax.fori_loop(1, TEAMS, scatter, 0)
+        own_pair = plane // 2
+        pairs = (own_pair, 1 - own_pair)
+
+        def half_rows(half):
+            return pl.ds(pl.multiple_of(pairs[half] * HALF, HALF), HALF)
+
+        def activate(half, layer=layer, base=base):
+            if half == 0:
+                take(layer, 3)
+                take(layer, 4)
+            gate_up = dot_f32(wgu_buf[layer], g_buf[half_rows(half), :], ((1,), (1,)))
+            act = (jax.nn.silu(gate_up[0:F_OWN]) * gate_up[F_OWN:]).astype(BF16)
+            own_hidden = a_all.at[layer, pl.ds(pl.multiple_of(slot * F_OWN, 16), F_OWN), half_rows(half)]
+            own_hidden[...] = act
+            gather_team(own_hidden, own_hidden, base + 3 + 2 * half)
+
+        gather_all(x_block, layer, norm_ffn[layer:layer + 1, :], activate)
+        for half in range(2):
+            wait_bytes(a_all.at[layer, 0:F_TEAM - F_OWN, 0:HALF], recv_sem.at[base + 3 + 2 * half])
+            if half == 0:
+                take(layer, 5)
+                wait_bytes(wd_buf.at[layer, 0:F_TEAM - F_OWN], down_recv.at[layer])
+            first = pairs[half] * (TEAMS // 2)
+            part[layer, pl.ds(first, TEAMS // 2)] = dot_f32(
+                a_all[layer, :, half_rows(half)], wd_buf[layer], ((0,), (0,))).reshape(TEAMS // 2, TEAM_ROWS, D_OWN)
+
+            def scatter(i, carry, first=first):
+                to = first + lax.rem(lax.rem(team, TEAMS // 2) + i, TEAMS // 2)
+                remote(part.at[layer, to], land.at[layer, team], send_sem.at[base + 4], recv_sem.at[base + 4],
+                       to * TEAM + slot).start()
+                return carry
+
+            lax.fori_loop(1 - half, TEAMS // 2, scatter, 0)
         pending.append((land.at[layer, 0:TEAMS - 1], send_sem.at[base + 4]))
         if layer + 1 < LAYERS:
             share_down(layer + 1)
@@ -274,11 +300,11 @@
         if layer == 0:
             own_block = xb_team.at[:, own_cols]
             own_block[...] = x_block
-            gather_team(own_block, own_block, 5)
-            wait_bytes(xb_team.at[:, 0:D - D_OWN], recv_sem.at[5])
+            gather_team(own_block, own_block, 6)
+            wait_bytes(xb_team.at[:, 0:D - D_OWN], recv_sem.at[6])
             x_team[...] = xb_team[...].astype(F32)
         else:
-            gather_all(x_block, LAYERS, norm_final[...])
+            gather_all(x_block, LAYERS, norm_final[...], lambda half: None)
 
     head_load.wait()
     copies = []
@@ -321,8 +347,7 @@
             pltpu.VMEM((VOCAB_OWN, ALL_ROWS), F32),
             pltpu.VMEM((O_ROWS, 32), BF16),
             pltpu.VMEM((HEADS * TEAM_ROWS, TEAM_ROWS * O_ROWS), BF16),
-            pltpu.VMEM((ROWS, D), F32),
-            pltpu.VMEM((TEAM, ROWS, D), F32),
+            pltpu.VMEM((TEAM, ROWS, D), BF16),
             pltpu.VMEM((TEAM_ROWS, D), F32),
             pltpu.VMEM((TEAM_ROWS, D), BF16),
             pltpu.VMEM((LAYERS, D, Q_OWN), BF16),
@@ -330,8 +355,8 @@
             pltpu.VMEM((LAYERS, HEADS * LATENT, D_OWN), BF16),
             pltpu.VMEM((LAYERS, 2 * F_OWN, D), BF16),
             pltpu.VMEM((LAYERS, F_TEAM, D_OWN), BF16),
-            pltpu.VMEM((LAYERS, TEAM, ROWS, Q_OWN), F32),
-            pltpu.VMEM((LAYERS, TEAM, ROWS, Q_OWN), F32),
+            pltpu.VMEM((LAYERS, TEAM, ROWS, Q_OWN), BF16),
+            pltpu.VMEM((LAYERS, TEAM, ROWS, Q_OWN), BF16),
             pltpu.VMEM((ROWS, 16, PAIR), F32),
             pltpu.VMEM((LAYERS, ROWS, O_ROWS, LATENT), BF16),
             pltpu.VMEM((LAYERS, TEAM, ROWS, O_ROWS, LATENT), BF16),
@@ -348,6 +373,7 @@
             dma((LAYERS + 1, 8)),
             dma((LAYERS,)),
             dma((LAYERS,)),
+            dma((LAYERS, ROWS, 2)),
             dma,
             dma((-(-VOCAB_OWN // HEAD_CHUNK),)),
         ],

time: 115 us -> 111 us (0.965)
  Pallas kernels: 112 us -> 108 us
    pallas_call x1, Pallas kernels: 112 us -> 108 us  [decode(): pl.pallas_call(decode_kernel, out_shape=jax.ShapeDtypeStruct((VOCAB_OWN,...]
where the time goes in v4:
time: 111 us; the launch traced here: 110 us
  Pallas kernels  108 us (97%)
  local copies, waits for them, and re-layouts  2.41 us (2%)
    pallas_call x1, Pallas kernels, decode(): pl.pallas_call(decode_kernel, out_shape=jax.ShapeDtypeStruct((VOCAB_OWN,...  108 us
    unnamed x1, local copies, waits for them, and re-layouts  2.41 us

profile of v4, /device:TPU:1, one launch (start us, length us, event | category | flops | bytes accessed | tf_op | source)
XLA Modules:
  0.0 110.4 jit_solution(10692364524450744565)
XLA Ops:
  0.0 108.0 %decode.1 = f32[1210,256]{1,0:T(8,128)} custom-call(bf16[2,2048]{1,0:T(2,128)(2,1)} %hidden.1, s32[2]{0:T(128)} %lengths.1, bf16[2,2,576,512]{3,2,1,0:T(8,128)(2,1)} %bitcast.8, f32[2,2048]{1,0:T(2,128)} %norm_attn.1, bf16[2,2048,11520]{2,1,0:T(8,128)(2,1)} %w_q.1, bf16[2,10240,2048]{2,1,0:T(8,128)(2,1)} %w_o.1, f32[2,2048]{1,0:T(2,128)} %norm_ffn.1, ...), custom_call_target="tpu_custom_call" | custom-call | tf_op jit(solution)/shard_map/decode/pallas_call | solution.py:340
  108.0 2.4 %copy.14 = f32[256,1210]{0,1:T(8,128)} copy(f32[256,1210]{0,1:T(8,128)} %bitcast.6) | data formatting | bytes 2478080

commit v5 on v4

--- a/solution.py
+++ b/solution.py
@@ -29,7 +29,8 @@
 PAIRS = HEADS // 2
 SHIFT = 64
 WIDE = KV + SHIFT
-O_ROWS = 24
+O_ROWS = 2 * HEADS
+O_COLS = LATENT // 2
 F_OWN = 80
 F_TEAM = F_OWN * TEAM
 VOCAB_OWN = 1210
@@ -64,10 +65,10 @@
     return pieces
 
 
-def decode_kernel(hidden, lengths, kv_cache, norm_attn, w_q, w_o, norm_ffn, w_gate, w_up, w_down, norm_final, w_head,
-                  out, head_buf, logits, pack, spread, hid_land, x_team, xb_team, wq_buf, kv_buf, wo_buf, wgu_buf, wd_buf,
+def decode_kernel(hidden_in, lengths_in, kv_cache, norm_attn_in, w_q, w_o, norm_ffn_in, w_gate, w_up, w_down, norm_final_in, w_head,
+                  out, hidden, lengths, norm_attn, norm_ffn, norm_final, head_buf, logits, pack, spread, hid_land, x_team, xb_team, wq_buf, kv_buf, wo_buf, wgu_buf, wd_buf,
                   q_send, q_land, q_pairs, o_send, o_land, o_heads, x_all, g_buf, a_all, part, land,
-                  load_sem, entry_sem, send_sem, recv_sem, plane_sem, down_send, down_recv, near_sem, head_sem, out_sem):
+                  load_sem, entry_sem, send_sem, recv_sem, plane_sem, down_send, down_recv, near_sem, head_sem, out_sem, small_sem):
     me = lax.axis_index('dp')
     team, slot = me // TEAM, lax.rem(me, TEAM)
     plane, core = team // 4, lax.rem(me, 2)
@@ -95,6 +96,12 @@
         return carry
 
     lax.fori_loop(1, TEAMS, greet, 0)
+
+    smalls = [pltpu.make_async_copy(src, dst, small_sem.at[i]) for i, (src, dst) in enumerate((
+        (hidden_in, hidden), (norm_attn_in, norm_attn), (lengths_in, lengths), (norm_ffn_in, norm_ffn),
+        (norm_final_in, norm_final)))]
+    for copy in smalls:
+        copy.start()
 
     loads = []
     for layer in range(LAYERS):
@@ -119,6 +126,8 @@
             kv_buf[layer, r, SHIFT + KV:, :] = jnp.zeros((SHIFT, SEQ), BF16)
     q_pairs[...] = jnp.zeros_like(q_pairs)
     make_selectors(pack, spread)
+    for copy in smalls:
+        copy.wait()
     hid_land[slot] = hidden[...]
 
     pl.semaphore_wait(barrier, TEAM - 1 + TEAMS - 1)
@@ -144,7 +153,7 @@
         mine[...] = block
         direct, passed = send_sem.at[16 + 2 * step], send_sem.at[17 + 2 * step]
         planes = (plane, plane + 1 - 2 * lax.rem(plane, 2), 3 - plane, lax.rem(plane + 2, 4))
-        for k in (3, 2, 1, 0):
+        for k in (1, 0, 3, 2) if step < LAYERS else (3, 2, 1, 0):
 
             def send(i, carry, k=k):
                 spot = lax.rem(lax.rem(me, 32) // 2 + 24 - i, 16)
@@ -229,7 +238,8 @@
             weights = jnp.exp(scores - jnp.max(scores, axis=-1, keepdims=True))
             probs = (weights / jnp.sum(weights, axis=-1, keepdims=True)).astype(BF16)
             context = dot_f32(probs, kv_buf[layer, r, SHIFT:SHIFT + LATENT, :], ((1,), (1,))).astype(BF16)
-            o_send[layer, r] = dot_f32(pack[...], context).astype(BF16)
+            halves = jnp.concatenate([context[:, :O_COLS], context[:, O_COLS:]], axis=0)
+            o_send[layer, r] = dot_f32(pack[...], halves).astype(BF16)
             block, dst = o_send.at[layer, r], o_land.at[layer, slot, r]
             osem, orecv = send_sem.at[base + 2], recv_sem.at[base + 2]
             for i in (4, 4 + 1 - 2 * core):
@@ -246,10 +256,10 @@
                 remote(piece, piece, send_sem.at[base + 2], recv_sem.at[base + 2], sibling).start()
         wait_bytes(o_land.at[layer, 0:TEAM - 3], recv_sem.at[base + 2])
 
-        o_heads[...] = dot_f32(spread[...], o_land[layer].reshape(TEAM_ROWS * O_ROWS, LATENT)).astype(BF16)
+        o_heads[...] = dot_f32(spread[...], o_land[layer].reshape(TEAM_ROWS * O_ROWS, O_COLS)).astype(BF16)
         take(layer, 2)
 
-        heads = jnp.concatenate([o_heads[i * TEAM_ROWS:(i + 1) * TEAM_ROWS, :] for i in range(HEADS)], axis=1)
+        heads = jnp.concatenate([o_heads[i * TEAM_ROWS:(i + 1) * TEAM_ROWS, :] for i in range(O_ROWS)], axis=1)
         delta = dot_f32(heads, wo_buf[layer])
         x_block = (x_block + delta).astype(BF16)
         if layer == 0:
@@ -322,31 +332,37 @@
 def make_selectors(pack, spread):
     row = lax.broadcasted_iota(jnp.int32, pack.shape, 0)
     col = lax.broadcasted_iota(jnp.int32, pack.shape, 1)
-    hit = (col == (row & 1) * 16 + (row >> 1)) & (row < HEADS)
+    half = jnp.where(row >= HEADS, 1, 0)
+    head = row - HEADS * half
+    hit = col == half * 32 + (head & 1) * 16 + (head >> 1)
     pack[...] = jnp.where(hit, 1.0, 0.0).astype(BF16)
     shape = (TEAM_ROWS, TEAM_ROWS * O_ROWS)
     row = lax.broadcasted_iota(jnp.int32, shape, 0)
     col = lax.broadcasted_iota(jnp.int32, shape, 1)
-    head = col - row * O_ROWS
-    for i in range(HEADS):
-        spread[i * TEAM_ROWS:(i + 1) * TEAM_ROWS, :] = jnp.where(head == i, 1.0, 0.0).astype(BF16)
+    at = col - row * O_ROWS
+    for i in range(O_ROWS):
+        wanted = (i % 2) * HEADS + i // 2
+        spread[i * TEAM_ROWS:(i + 1) * TEAM_ROWS, :] = jnp.where(at == wanted, 1.0, 0.0).astype(BF16)
 
 
 def decode(hidden, lengths, kv_cache, norm_attn, w_q, w_o, norm_ffn, w_gate, w_up, w_down, norm_final, w_head):
-    vmem = pl.BlockSpec(memory_space=pltpu.VMEM)
-    smem = pl.BlockSpec(memory_space=pltpu.SMEM)
     hbm = pl.BlockSpec(memory_space=pl.ANY)
     dma = pltpu.SemaphoreType.DMA
     return pl.pallas_call(
         decode_kernel,
         out_shape=jax.ShapeDtypeStruct((VOCAB_OWN, ALL_ROWS), F32),
-        in_specs=[vmem, smem, hbm, vmem, hbm, hbm, vmem, hbm, hbm, hbm, vmem, hbm],
+        in_specs=[hbm] * 12,
         out_specs=hbm,
         scratch_shapes=[
+            pltpu.VMEM((ROWS, D), BF16),
+            pltpu.SMEM((ROWS,), jnp.int32),
+            pltpu.VMEM((LAYERS, D), F32),
+            pltpu.VMEM((LAYERS, D), F32),
+            pltpu.VMEM((1, D), F32),
             pltpu.VMEM((VOCAB_OWN, D), BF16),
             pltpu.VMEM((VOCAB_OWN, ALL_ROWS), F32),
-            pltpu.VMEM((O_ROWS, 32), BF16),
-            pltpu.VMEM((HEADS * TEAM_ROWS, TEAM_ROWS * O_ROWS), BF16),
+            pltpu.VMEM((O_ROWS, 64), BF16),
+            pltpu.VMEM((O_ROWS * TEAM_ROWS, TEAM_ROWS * O_ROWS), BF16),
             pltpu.VMEM((TEAM, ROWS, D), BF16),
             pltpu.VMEM((TEAM_ROWS, D), F32),
             pltpu.VMEM((TEAM_ROWS, D), BF16),
@@ -358,9 +374,9 @@
             pltpu.VMEM((LAYERS, TEAM, ROWS, Q_OWN), BF16),
             pltpu.VMEM((LAYERS, TEAM, ROWS, Q_OWN), BF16),
             pltpu.VMEM((ROWS, 16, PAIR), F32),
-            pltpu.VMEM((LAYERS, ROWS, O_ROWS, LATENT), BF16),
-            pltpu.VMEM((LAYERS, TEAM, ROWS, O_ROWS, LATENT), BF16),
-            pltpu.VMEM((HEADS * TEAM_ROWS, LATENT), BF16),
+            pltpu.VMEM((LAYERS, ROWS, O_ROWS, O_COLS), BF16),
+            pltpu.VMEM((LAYERS, TEAM, ROWS, O_ROWS, O_COLS), BF16),
+            pltpu.VMEM((O_ROWS * TEAM_ROWS, O_COLS), BF16),
             pltpu.VMEM((LAYERS + 1, TEAMS, TEAM_ROWS, D), BF16),
             pltpu.VMEM((ALL_ROWS, D), BF16),
             pltpu.VMEM((LAYERS, F_TEAM, ALL_ROWS), BF16),
@@ -376,6 +392,7 @@
             dma((LAYERS, ROWS, 2)),
             dma,
             dma((-(-VOCAB_OWN // HEAD_CHUNK),)),
+            dma((5,)),
         ],
         compiler_params=pltpu.CompilerParams(collective_id=0, has_side_effects=True, vmem_limit_bytes=60 * 1024 * 1024),
         name='decode',

time: 111 us -> 110 us (level)
  no operation moved by 1% of the time
where the time goes in v5:
time: 110 us
  Pallas kernels  108 us (98%)
  local copies, waits for them, and re-layouts  2.41 us (2%)
    pallas_call x1, Pallas kernels, decode(): pl.pallas_call(decode_kernel, out_shape=jax.ShapeDtypeStruct((VOCAB_OWN,...  108 us
    unnamed x1, local copies, waits for them, and re-layouts  2.41 us

profile of v5, /device:TPU:1, one launch (start us, length us, event | category | flops | bytes accessed | tf_op | source)
XLA Modules:
  0.0 110.3 jit_solution(8098952610580823072)
XLA Ops:
  0.0 107.9 %decode.1 = f32[1210,256]{1,0:T(8,128)} custom-call(bf16[2,2048]{1,0:T(2,128)(2,1)} %hidden_in.1, s32[2]{0:T(128)} %lengths_in.1, bf16[2,2,576,512]{3,2,1,0:T(8,128)(2,1)} %bitcast.8, f32[2,2048]{1,0:T(2,128)} %norm_attn_in.1, bf16[2,2048,11520]{2,1,0:T(8,128)(2,1)} %w_q.1, bf16[2,10240,2048]{2,1,0:T(8,128)(2,1)} %w_o.1, f32[2,2048]{1,0:T(2,128)} %norm_ffn_in.1, ...), custom_call_target="tpu_custom_call" | custom-call | tf_op jit(solution)/shard_map/decode/pallas_call | solution.py:351
  107.9 2.4 %copy.14 = f32[256,1210]{0,1:T(8,128)} copy(f32[256,1210]{0,1:T(8,128)} %bitcast.6) | data formatting | bytes 2478080

commit v6 on v5

--- a/solution.py
+++ b/solution.py
@@ -65,10 +65,10 @@
     return pieces
 
 
-def decode_kernel(hidden_in, lengths_in, kv_cache, norm_attn_in, w_q, w_o, norm_ffn_in, w_gate, w_up, w_down, norm_final_in, w_head,
-                  out, hidden, lengths, norm_attn, norm_ffn, norm_final, head_buf, logits, pack, spread, hid_land, x_team, xb_team, wq_buf, kv_buf, wo_buf, wgu_buf, wd_buf,
+def decode_kernel(hidden, lengths, kv_cache, norm_attn, w_q, w_o, norm_ffn, w_gate, w_up, w_down, norm_final, w_head,
+                  out, head_buf, logits, pack, spread, hid_land, x_team, xb_team, wq_buf, kv_buf, wo_buf, wgu_buf, wd_buf,
                   q_send, q_land, q_pairs, o_send, o_land, o_heads, x_all, g_buf, a_all, part, land,
-                  load_sem, entry_sem, send_sem, recv_sem, plane_sem, down_send, down_recv, near_sem, head_sem, out_sem, small_sem):
+                  load_sem, entry_sem, send_sem, recv_sem, plane_sem, down_send, down_recv, near_sem, head_sem, out_sem):
     me = lax.axis_index('dp')
     team, slot = me // TEAM, lax.rem(me, TEAM)
     plane, core = team // 4, lax.rem(me, 2)
@@ -96,12 +96,6 @@
         return carry
 
     lax.fori_loop(1, TEAMS, greet, 0)
-
-    smalls = [pltpu.make_async_copy(src, dst, small_sem.at[i]) for i, (src, dst) in enumerate((
-        (hidden_in, hidden), (norm_attn_in, norm_attn), (lengths_in, lengths), (norm_ffn_in, norm_ffn),
-        (norm_final_in, norm_final)))]
-    for copy in smalls:
-        copy.start()
 
     loads = []
     for layer in range(LAYERS):
@@ -126,8 +120,6 @@
             kv_buf[layer, r, SHIFT + KV:, :] = jnp.zeros((SHIFT, SEQ), BF16)
     q_pairs[...] = jnp.zeros_like(q_pairs)
     make_selectors(pack, spread)
-    for copy in smalls:
-        copy.wait()
     hid_land[slot] = hidden[...]
 
     pl.semaphore_wait(barrier, TEAM - 1 + TEAMS - 1)
@@ -153,7 +145,7 @@
         mine[...] = block
         direct, passed = send_sem.at[16 + 2 * step], send_sem.at[17 + 2 * step]
         planes = (plane, plane + 1 - 2 * lax.rem(plane, 2), 3 - plane, lax.rem(plane + 2, 4))
-        for k in (1, 0, 3, 2) if step < LAYERS else (3, 2, 1, 0):
+        for k in (1, 0, 3, 2):
 
             def send(i, carry, k=k):
                 spot = lax.rem(lax.rem(me, 32) // 2 + 24 - i, 16)
@@ -242,19 +234,18 @@
             o_send[layer, r] = dot_f32(pack[...], halves).astype(BF16)
             block, dst = o_send.at[layer, r], o_land.at[layer, slot, r]
             osem, orecv = send_sem.at[base + 2], recv_sem.at[base + 2]
-            for i in (4, 4 + 1 - 2 * core):
-                remote(block, dst, osem, orecv, mate(i)).start()
+            remote(block, dst, osem, near_sem.at[layer, r, 2], mate(4)).start()
             remote(block, dst, osem, near_sem.at[layer, r, 0], mate(2)).start()
             remote(block, dst, osem, near_sem.at[layer, r, 1], mate(TEAM - 2)).start()
             remote(block, dst, osem, orecv, sibling).start()
             o_land[layer, slot, r] = o_send[layer, r]
             pending.extend([(block, osem)] * (TEAM - 1))
         for r in range(ROWS):
-            for side, i in enumerate((TEAM - 2, 2)):
+            for side, i in enumerate((TEAM - 2, 2, 4)):
                 piece = o_land.at[layer, lax.rem(slot + i, TEAM), r]
                 wait_bytes(piece, near_sem.at[layer, r, side])
                 remote(piece, piece, send_sem.at[base + 2], recv_sem.at[base + 2], sibling).start()
-        wait_bytes(o_land.at[layer, 0:TEAM - 3], recv_sem.at[base + 2])
+        wait_bytes(o_land.at[layer, 0:TEAM // 2], recv_sem.at[base + 2])
 
         o_heads[...] = dot_f32(spread[...], o_land[layer].reshape(TEAM_ROWS * O_ROWS, O_COLS)).astype(BF16)
         take(layer, 2)
@@ -346,19 +337,16 @@
 
 
 def decode(hidden, lengths, kv_cache, norm_attn, w_q, w_o, norm_ffn, w_gate, w_up, w_down, norm_final, w_head):
+    vmem = pl.BlockSpec(memory_space=pltpu.VMEM)
+    smem = pl.BlockSpec(memory_space=pltpu.SMEM)
     hbm = pl.BlockSpec(memory_space=pl.ANY)
     dma = pltpu.SemaphoreType.DMA
     return pl.pallas_call(
         decode_kernel,
         out_shape=jax.ShapeDtypeStruct((VOCAB_OWN, ALL_ROWS), F32),
-        in_specs=[hbm] * 12,
+        in_specs=[vmem, smem, hbm, vmem, hbm, hbm, vmem, hbm, hbm, hbm, vmem, hbm],
         out_specs=hbm,
         scratch_shapes=[
-            pltpu.VMEM((ROWS, D), BF16),
-            pltpu.SMEM((ROWS,), jnp.int32),
-            pltpu.VMEM((LAYERS, D), F32),
-            pltpu.VMEM((LAYERS, D), F32),
-            pltpu.VMEM((1, D), F32),
             pltpu.VMEM((VOCAB_OWN, D), BF16),
             pltpu.VMEM((VOCAB_OWN, ALL_ROWS), F32),
             pltpu.VMEM((O_ROWS, 64), BF16),
@@ -389,10 +377,9 @@
             dma((LAYERS + 1, 8)),
             dma((LAYERS,)),
             dma((LAYERS,)),
-            dma((LAYERS, ROWS, 2)),
+            dma((LAYERS, ROWS, 3)),
             dma,
             dma((-(-VOCAB_OWN // HEAD_CHUNK),)),
-            dma((5,)),
         ],
         compiler_params=pltpu.CompilerParams(collective_id=0, has_side_effects=True, vmem_limit_bytes=60 * 1024 * 1024),
         name='decode',

time: 110 us -> 105 us (0.955)
  Pallas kernels: 108 us -> 103 us
    pallas_call x1, Pallas kernels: 108 us -> 103 us  [decode(): pl.pallas_call(decode_kernel, out_shape=jax.ShapeDtypeStruct((VOCAB_OWN,...]
where the time goes in v6:
time: 105 us
  Pallas kernels  103 us (98%)
  local copies, waits for them, and re-layouts  2.41 us (2%)
    pallas_call x1, Pallas kernels, decode(): pl.pallas_call(decode_kernel, out_shape=jax.ShapeDtypeStruct((VOCAB_OWN,...  103 us
    unnamed x1, local copies, waits for them, and re-layouts  2.41 us

profile of v6, /device:TPU:1, one launch (start us, length us, event | category | flops | bytes accessed | tf_op | source)
XLA Modules:
  0.0 105.1 jit_solution(11074019554053034078)
XLA Ops:
  0.0 102.7 %decode.1 = f32[1210,256]{1,0:T(8,128)} custom-call(bf16[2,2048]{1,0:T(2,128)(2,1)} %hidden.1, s32[2]{0:T(128)} %lengths.1, bf16[2,2,576,512]{3,2,1,0:T(8,128)(2,1)} %bitcast.8, f32[2,2048]{1,0:T(2,128)} %norm_attn.1, bf16[2,2048,11520]{2,1,0:T(8,128)(2,1)} %w_q.1, bf16[2,10240,2048]{2,1,0:T(8,128)(2,1)} %w_o.1, f32[2,2048]{1,0:T(2,128)} %norm_ffn.1, ...), custom_call_target="tpu_custom_call" | custom-call | tf_op jit(solution)/shard_map/decode/pallas_call | solution.py:344
  102.7 2.4 %copy.14 = f32[256,1210]{0,1:T(8,128)} copy(f32[256,1210]{0,1:T(8,128)} %bitcast.6) | data formatting | bytes 2478080

commit v7 on v5

--- a/solution.py
+++ b/solution.py
@@ -102,6 +102,10 @@
         (norm_final_in, norm_final)))]
     for copy in smalls:
         copy.start()
+    q_pairs[...] = jnp.zeros_like(q_pairs)
+    make_selectors(pack, spread)
+    for copy in smalls:
+        copy.wait()
 
     loads = []
     for layer in range(LAYERS):
@@ -124,10 +128,6 @@
         for r in range(ROWS):
             kv_buf[layer, r, 0:SHIFT, :] = jnp.zeros((SHIFT, SEQ), BF16)
             kv_buf[layer, r, SHIFT + KV:, :] = jnp.zeros((SHIFT, SEQ), BF16)
-    q_pairs[...] = jnp.zeros_like(q_pairs)
-    make_selectors(pack, spread)
-    for copy in smalls:
-        copy.wait()
     hid_land[slot] = hidden[...]
 
     pl.semaphore_wait(barrier, TEAM - 1 + TEAMS - 1)
@@ -153,7 +153,7 @@
         mine[...] = block
         direct, passed = send_sem.at[16 + 2 * step], send_sem.at[17 + 2 * step]
         planes = (plane, plane + 1 - 2 * lax.rem(plane, 2), 3 - plane, lax.rem(plane + 2, 4))
-        for k in (1, 0, 3, 2) if step < LAYERS else (3, 2, 1, 0):
+        for k in (1, 0, 3, 2):
 
             def send(i, carry, k=k):
                 spot = lax.rem(lax.rem(me, 32) // 2 + 24 - i, 16)
@@ -242,19 +242,18 @@
             o_send[layer, r] = dot_f32(pack[...], halves).astype(BF16)
             block, dst = o_send.at[layer, r], o_land.at[layer, slot, r]
             osem, orecv = send_sem.at[base + 2], recv_sem.at[base + 2]
-            for i in (4, 4 + 1 - 2 * core):
-                remote(block, dst, osem, orecv, mate(i)).start()
+            remote(block, dst, osem, near_sem.at[layer, r, 2], mate(4)).start()
             remote(block, dst, osem, near_sem.at[layer, r, 0], mate(2)).start()
             remote(block, dst, osem, near_sem.at[layer, r, 1], mate(TEAM - 2)).start()
             remote(block, dst, osem, orecv, sibling).start()
             o_land[layer, slot, r] = o_send[layer, r]
             pending.extend([(block, osem)] * (TEAM - 1))
         for r in range(ROWS):
-            for side, i in enumerate((TEAM - 2, 2)):
+            for side, i in enumerate((TEAM - 2, 2, 4)):
                 piece = o_land.at[layer, lax.rem(slot + i, TEAM), r]
                 wait_bytes(piece, near_sem.at[layer, r, side])
                 remote(piece, piece, send_sem.at[base + 2], recv_sem.at[base + 2], sibling).start()
-        wait_bytes(o_land.at[layer, 0:TEAM - 3], recv_sem.at[base + 2])
+        wait_bytes(o_land.at[layer, 0:TEAM // 2], recv_sem.at[base + 2])
 
         o_heads[...] = dot_f32(spread[...], o_land[layer].reshape(TEAM_ROWS * O_ROWS, O_COLS)).astype(BF16)
         take(layer, 2)
@@ -291,7 +290,7 @@
                 a_all[layer, :, half_rows(half)], wd_buf[layer], ((0,), (0,))).reshape(TEAMS // 2, TEAM_ROWS, D_OWN)
 
             def scatter(i, carry, first=first):
-                to = first + lax.rem(lax.rem(team, TEAMS // 2) + i, TEAMS // 2)
+                to = first + lax.rem(lax.rem(team, TEAMS // 2) + TEAMS // 2 - i, TEAMS // 2)
                 remote(part.at[layer, to], land.at[layer, team], send_sem.at[base + 4], recv_sem.at[base + 4],
                        to * TEAM + slot).start()
                 return carry
@@ -389,7 +388,7 @@
             dma((LAYERS + 1, 8)),
             dma((LAYERS,)),
             dma((LAYERS,)),
-            dma((LAYERS, ROWS, 2)),
+            dma((LAYERS, ROWS, 3)),
             dma,
             dma((-(-VOCAB_OWN // HEAD_CHUNK),)),
             dma((5,)),

time: 110 us -> 104 us (0.945)
  Pallas kernels: 108 us -> 101 us
    pallas_call x1, Pallas kernels: 108 us -> 101 us  [decode(): pl.pallas_call(decode_kernel, out_shape=jax.ShapeDtypeStruct((VOCAB_OWN,...]
where the time goes in v7:
time: 104 us
  Pallas kernels  101 us (97%)
  local copies, waits for them, and re-layouts  2.41 us (2%)
    pallas_call x1, Pallas kernels, decode(): pl.pallas_call(decode_kernel, out_shape=jax.ShapeDtypeStruct((VOCAB_OWN,...  101 us
    unnamed x1, local copies, waits for them, and re-layouts  2.41 us

profile of v7, /device:TPU:1, one launch (start us, length us, event | category | flops | bytes accessed | tf_op | source)
XLA Modules:
  0.0 103.5 jit_solution(578789432125666838)
XLA Ops:
  0.0 101.1 %decode.1 = f32[1210,256]{1,0:T(8,128)} custom-call(bf16[2,2048]{1,0:T(2,128)(2,1)} %hidden_in.1, s32[2]{0:T(128)} %lengths_in.1, bf16[2,2,576,512]{3,2,1,0:T(8,128)(2,1)} %bitcast.8, f32[2,2048]{1,0:T(2,128)} %norm_attn_in.1, bf16[2,2048,11520]{2,1,0:T(8,128)(2,1)} %w_q.1, bf16[2,10240,2048]{2,1,0:T(8,128)(2,1)} %w_o.1, f32[2,2048]{1,0:T(2,128)} %norm_ffn_in.1, ...), custom_call_target="tpu_custom_call" | custom-call | tf_op jit(solution)/shard_map/decode/pallas_call | solution.py:350
  101.1 2.4 %copy.14 = f32[256,1210]{0,1:T(8,128)} copy(f32[256,1210]{0,1:T(8,128)} %bitcast.6) | data formatting | bytes 2478080
